TPU v7x, 16 devices: a whole 2x2x2 slice. The times are simulated.
16 devices in a mesh: tp: 4 (over z, y), cp: 4 (over x, core).
Axes of the slice: x: 2, y: 2, z: 2, core: 2. Of those that a mesh axis runs over, the one named last changes fastest.
Arguments:
- x_in: bfloat16 [8192, 2048], P('cp')
- positions: int32 [8192], P('cp')
- attn_gain: bfloat16 [2, 2048], replicated
- mlp_gain: bfloat16 [2, 2048], replicated
- w_query: bfloat16 [2, 2048, 2048], P(None, None, 'tp')
- b_query: bfloat16 [2, 2048], P(None, 'tp')
- w_key: bfloat16 [2, 2048, 2048], P(None, None, 'tp')
- b_key: bfloat16 [2, 2048], P(None, 'tp')
- w_value: bfloat16 [2, 2048, 2048], P(None, None, 'tp')
- b_value: bfloat16 [2, 2048], P(None, 'tp')
- w_out: bfloat16 [2, 2048, 2048], P(None, 'tp')
- w_gate: bfloat16 [2, 2048, 5504], P(None, None, 'tp')
- w_up: bfloat16 [2, 2048, 5504], P(None, None, 'tp')
- w_down: bfloat16 [2, 5504, 2048], P(None, 'tp')
Outputs:
- output 1: bfloat16 [8192, 2048], P('cp')
- output 2: bfloat16 [8192, 16, 128], P('cp', 'tp')
- output 3: bfloat16 [8192, 16, 128], P('cp', 'tp')
- output 4: bfloat16 [8192, 16, 128], P('cp', 'tp')
- output 5: bfloat16 [8192, 16, 128], P('cp', 'tp')
All inputs are finite; a program needn't handle non-finite values.
Results may differ from a plain program's by a relative error of at most 0.02.
Values are sent between devices in bfloat16 or wider.
A program may use at most 1 GiB of HBM per device.

v0:
```python
import functools

import jax
import jax.numpy as jnp
from jax import lax
from jax.experimental import pallas as pl
from jax.experimental.pallas import tpu as pltpu
from jax.sharding import PartitionSpec as P


HEAD_DIM = 128
WINDOW = 4096
NEG = -1e37
EXP_SCALE = HEAD_DIM ** -0.5 * 1.4426950408889634


def flash_kernel(n_src, window, bq, bk, chains, fresh, final, deltas, q_ref, *refs):
    kv = refs[:2 * n_src]
    refs = refs[2 * n_src:]
    if not fresh:
        acc_in, ml_in = refs[:2]
        refs = refs[2:]
    if final:
        o_ref = refs[0]
        refs = refs[1:]
    else:
        acc_out, ml_out = refs[:2]
        refs = refs[2:]
    vts = refs[:n_src]
    acc, stat, s_a, s_b, p_a, p_b = refs[n_src:]
    s_bufs, p_bufs = (s_a, s_b), (p_a, p_b)
    i = pl.program_id(1)
    tk = kv[0].shape[0]

    @pl.when(i == 0)
    def _():
        for n in range(n_src):
            vts[n][...] = kv[2 * n + 1][...].T

    if fresh:
        acc[...] = jnp.zeros_like(acc)
        stat[0:1, :] = jnp.full((1, bq), NEG, jnp.float32)
        stat[1:2, :] = jnp.zeros((1, bq), jnp.float32)
    else:
        acc[...] = acc_in[...]
        stat[0:2, :] = ml_in[0, 0:2, :]
    t0 = i * bq
    cw = bq // chains
    kc, ec = 256, 32
    parts = bk // kc

    def step(k_ref, vt, delta, j, masked):
        off = pl.multiple_of(j * bk, bk)

        def scores(c, r):
            kb = k_ref[pl.ds(off + r * kc, kc), :]
            s = lax.dot_general(kb, q_ref[c * cw:(c + 1) * cw, :], (((1,), (1,)), ((), ())), preferred_element_type=jnp.float32)
            if masked:
                rel = lax.broadcasted_iota(jnp.int32, (kc, cw), 0) - lax.broadcasted_iota(jnp.int32, (kc, cw), 1) + (delta + off + r * kc - t0 - c * cw)
                s = jnp.where((rel <= 0) & (rel > -window), s, NEG)
            s_bufs[c % 2][r * kc:(r + 1) * kc, :] = s
            return jnp.max(s.reshape(kc // 8, 8, cw), axis=0)

        def weigh(c, alpha):
            sl = slice(c * cw, (c + 1) * cw)
            acc[:, sl] = acc[:, sl] * alpha + jnp.dot(vt[:, pl.ds(off, bk)], p_bufs[c % 2][...], preferred_element_type=jnp.float32)

        top = functools.reduce(jnp.maximum, [scores(0, r) for r in range(parts)])
        pending = None
        for c in range(chains):
            sl = slice(c * cw, (c + 1) * cw)
            m_prev = stat[0:1, sl]
            m_new = jnp.maximum(m_prev, jnp.max(top, axis=0, keepdims=True))
            alpha = jnp.exp2((m_prev - m_new) * EXP_SCALE)
            stat[0:1, sl] = m_new
            tops, total = [], None
            for r in range(parts):
                if c + 1 < chains:
                    tops.append(scores(c + 1, r))
                for e in range(r * kc, (r + 1) * kc, ec):
                    p = jnp.exp2((s_bufs[c % 2][e:e + ec, :] - m_new) * EXP_SCALE)
                    p_bufs[c % 2][e:e + ec, :] = p.astype(jnp.bfloat16)
                    part = jnp.sum(p.reshape(ec // 8, 8, cw), axis=0)
                    total = part if total is None else total + part
                if r == 0 and pending is not None:
                    weigh(*pending)
            stat[1:2, sl] = stat[1:2, sl] * alpha + jnp.sum(total, axis=0, keepdims=True)
            pending = (c, alpha)
            if tops:
                top = functools.reduce(jnp.maximum, tops)
        weigh(*pending)

    nk = tk // bk
    for n in range(n_src):
        delta = deltas[n]
        hi_any = jnp.clip((t0 + bq - 1 - delta) // bk + 1, 0, nk)
        hi_full = jnp.clip((t0 + 1 - delta) // bk, 0, nk)
        lo_any = jnp.clip((t0 - window + 1 - delta) // bk, 0, nk)
        lo_full = jnp.clip((t0 + bq - window - delta + bk - 1) // bk, 0, nk)
        lo_full = jnp.minimum(lo_full, hi_any)
        hi_full = jnp.maximum(hi_full, lo_full)

        def body(masked):
            def f(j, _):
                step(kv[2 * n], vts[n], delta, j, masked)
                return 0

            return f

        lax.fori_loop(lo_any, lo_full, body(True), 0)
        lax.fori_loop(lo_full, hi_full, body(False), 0)
        lax.fori_loop(hi_full, hi_any, body(True), 0)
    if final:
        o_ref[...] = (acc[...] * (1.0 / stat[1:2, :])).T.astype(o_ref.dtype)
    else:
        acc_out[...] = acc[...]
        ml_out[0, 0:2, :] = stat[0:2, :]


def flash(q, sources, deltas, window, first, count, carry=None, start=0, final=True, bq=1024, bk=1024, chains=4, units=1.0):
    tq = q.shape[0]
    width = count * HEAD_DIM
    tk = sources[0].shape[0]
    pair = sources[0].shape[1] // (2 * HEAD_DIM)
    n_src = len(sources)
    k_spec = pl.BlockSpec((tk, HEAD_DIM), lambda h, i, d: (0, (first + h) % pair))
    v_spec = pl.BlockSpec((tk, HEAD_DIM), lambda h, i, d: (0, pair + (first + h) % pair))
    in_specs = [pl.BlockSpec((bq, HEAD_DIM), lambda h, i, d: (i, first + h))]
    args = [q]
    for source in sources:
        in_specs += [k_spec, v_spec]
        args += [source, source]
    if carry is not None:
        in_specs += [pl.BlockSpec((HEAD_DIM, bq), lambda h, i, d: (start + h, i)), pl.BlockSpec((1, 8, bq), lambda h, i, d: (start + h, 0, i))]
        args += list(carry)
    if final:
        out_shape = jax.ShapeDtypeStruct((tq, width), jnp.bfloat16)
        out_specs = pl.BlockSpec((bq, HEAD_DIM), lambda h, i, d: (i, h))
    else:
        out_shape = (jax.ShapeDtypeStruct((width, tq), jnp.float32), jax.ShapeDtypeStruct((count, 8, tq), jnp.float32))
        out_specs = (pl.BlockSpec((HEAD_DIM, bq), lambda h, i, d: (h, i)), pl.BlockSpec((1, 8, bq), lambda h, i, d: (h, 0, i)))
    result = pl.pallas_call(
        functools.partial(flash_kernel, n_src, window, bq, bk, chains, carry is None, final),
        out_shape=out_shape,
        grid_spec=pltpu.PrefetchScalarGridSpec(
            num_scalar_prefetch=1, grid=(count, tq // bq), in_specs=in_specs, out_specs=out_specs,
            scratch_shapes=[pltpu.VMEM((HEAD_DIM, tk), jnp.bfloat16)] * n_src + [pltpu.VMEM((HEAD_DIM, bq), jnp.float32), pltpu.VMEM((8, bq), jnp.float32)]
            + [pltpu.VMEM((bk, bq // chains), jnp.float32)] * 2 + [pltpu.VMEM((bk, bq // chains), jnp.bfloat16)] * 2),
        compiler_params=pltpu.CompilerParams(dimension_semantics=("arbitrary", "arbitrary"), vmem_limit_bytes=48 << 20),
        cost_estimate=pl.CostEstimate(flops=int(units * 4 * tq * tk * width), bytes_accessed=8 * tq * width, transcendentals=int(units * tq * tk * count)),
    )(deltas, *args)
    return result if final else list(result)


def mlp_kernel(tile, first_ref, h_ref, a_ref, b_ref, mine_ref, other_ref, *refs):
    res_ref = refs[0] if len(refs) == 3 else None
    o_ref, acc = refs[-2:]
    step = pl.program_id(0)
    core = first_ref[0]
    half = mine_ref.shape[2]

    @pl.when(step == 0)
    def _():
        if res_ref is None:
            acc[...] = jnp.zeros_like(acc)
        else:
            acc[...] = res_ref[...].astype(jnp.float32)

    across = (((1,), (1,)), ((), ()))
    for r in range(h_ref.shape[0] // tile):
        rows = slice(r * tile, (r + 1) * tile)
        h = h_ref[rows, :]
        a = lax.dot_general(h, a_ref[0], across, preferred_element_type=jnp.float32)
        b = lax.dot_general(h, b_ref[0], across, preferred_element_type=jnp.float32)
        gate = jnp.where(core == 0, a, b)
        up = jnp.where(core == 0, b, a)
        act = (gate * (1.0 / (1.0 + jnp.exp(-gate))) * up).astype(jnp.bfloat16)
        for ref, place in ((mine_ref, core), (other_ref, 1 - core)):
            cols = pl.ds(pl.multiple_of(place * half, half), half)
            acc[rows, cols] += jnp.dot(act, ref[0], preferred_element_type=jnp.float32)

    @pl.when(step == pl.num_programs(0) - 1)
    def _():
        o_ref[...] = acc[...].astype(o_ref.dtype)


def mlp(core, hidden, w_a, w_b, d_mine, d_other, residual=None, tile=256):
    rows, width = hidden.shape
    shards, cols, _ = w_a.shape
    half = d_mine.shape[2]
    out_type = jnp.bfloat16 if residual is None else jnp.float32
    whole = pl.BlockSpec((rows, width), lambda s, c: (0, 0))
    wide = pl.BlockSpec((1, cols, width), lambda s, c: (s, 0, 0))
    down = pl.BlockSpec((1, cols, half), lambda s, c: (s, 0, 0))
    args = [hidden, w_a, w_b, d_mine, d_other] + ([] if residual is None else [residual])
    return pl.pallas_call(
        functools.partial(mlp_kernel, min(tile, rows)),
        out_shape=jax.ShapeDtypeStruct((rows, width), out_type),
        grid_spec=pltpu.PrefetchScalarGridSpec(
            num_scalar_prefetch=1, grid=(shards,),
            in_specs=[whole, wide, wide, down, down] + ([] if residual is None else [whole]),
            out_specs=whole,
            scratch_shapes=[pltpu.VMEM((rows, width), jnp.float32)]),
        compiler_params=pltpu.CompilerParams(dimension_semantics=("arbitrary",), vmem_limit_bytes=56 << 20),
        cost_estimate=pl.CostEstimate(flops=6 * rows * width * cols * shards, bytes_accessed=6 * width * cols * shards, transcendentals=rows * cols * shards),
    )(core, *args)


def select_piece(step, pieces, x_buf):
    whole, halves = pieces[:-2], pieces[-2:]
    for d, ref in enumerate(whole):
        @pl.when(step == d)
        def _():
            x_buf[...] = ref[...]

    @pl.when(step == len(whole))
    def _():
        rows = halves[0].shape[0]
        x_buf[:rows, :] = halves[0][...]
        x_buf[rows:, :] = halves[1][...]


def qkv_kernel(layer, norm, n_pieces, place_ref, *refs):
    pieces, refs = refs[:n_pieces], refs[n_pieces:]
    gain_ref, wq, wk, wv, bq, bk, bv, cos_ref, sin_ref = refs[:9]
    if n_pieces > 1:
        q_ref, kv0_ref, kv1_ref, x_buf = refs[-4:]
        select_piece(pl.program_id(0), pieces, x_buf)
        x = x_buf[...]
    else:
        q_ref, kv0_ref, kv1_ref = refs[-3:]
        x = pieces[0][...]
    if norm:
        xf = x.astype(jnp.float32)
        x = (xf * lax.rsqrt(jnp.mean(xf * xf, axis=-1, keepdims=True) + 1e-6) * gain_ref[layer:layer + 1, :].astype(jnp.float32)).astype(jnp.bfloat16)
    cos, sin = cos_ref[...], sin_ref[...]
    kv = (kv0_ref, kv1_ref)
    width = wq.shape[2]
    pair = kv0_ref.shape[1] // 2
    for w_ref, b_ref, kind in ((wk, bk, 1), (wv, bv, 2), (wq, bq, 0)):
        out = jnp.dot(x, w_ref[0], preferred_element_type=jnp.float32) + b_ref[layer:layer + 1, :].astype(jnp.float32)
        for h in range(width // HEAD_DIM):
            part = out[:, h * HEAD_DIM:(h + 1) * HEAD_DIM]
            if kind != 2:
                part = part * cos + pltpu.roll(part, HEAD_DIM // 2, 1) * sin
            part = part.astype(jnp.bfloat16)
            if kind == 0:
                q_ref[:, h * HEAD_DIM:(h + 1) * HEAD_DIM] = part
            else:
                at = (kind - 1) * pair + (h * HEAD_DIM) % pair
                kv[h * HEAD_DIM // pair][:, at:at + HEAD_DIM] = part


def piece_specs(pieces, tile):
    if len(pieces) == 1:
        return [pl.BlockSpec((tile, pieces[0].shape[1]), lambda i, p: (i, 0))]
    return [pl.BlockSpec(x.shape, lambda i, p: (0, 0)) for x in pieces]


def qkv(layer, norm, place, pieces, gain, weights, biases, cos, sin, block, prior=None, tile=256):
    width = pieces[0].shape[1]
    out_width = weights[0].shape[2]
    steps = place.shape[0]
    spot = lambda i, p: (p[i], 0)
    fixed = lambda shape: pl.BlockSpec(shape, lambda i, p: (0, 0))
    in_specs = piece_specs(pieces, tile) + [fixed(gain.shape)]
    in_specs += [pl.BlockSpec((1, width, out_width), lambda i, p: (layer, 0, 0))] * 3
    in_specs += [fixed(biases[0].shape)] * 3
    in_specs += [pl.BlockSpec((tile, HEAD_DIM), spot)] * 2
    args = [*pieces, gain, *weights, *biases, cos, sin]
    aliases = {}
    if prior is not None:
        aliases = {1 + len(args) + k: k for k in range(3)}
        in_specs += [pl.BlockSpec(memory_space=pl.ANY)] * 3
        args += list(prior)
    return pl.pallas_call(
        functools.partial(qkv_kernel, layer, norm, len(pieces)),
        out_shape=tuple(jax.ShapeDtypeStruct((block, out_width), jnp.bfloat16) for _ in range(3)),
        grid_spec=pltpu.PrefetchScalarGridSpec(
            num_scalar_prefetch=1, grid=(steps,), in_specs=in_specs,
            out_specs=tuple(pl.BlockSpec((tile, out_width), spot) for _ in range(3)),
            scratch_shapes=[pltpu.VMEM((tile, width), jnp.bfloat16)] if len(pieces) > 1 else []),
        input_output_aliases=aliases,
        compiler_params=pltpu.CompilerParams(dimension_semantics=("arbitrary",), vmem_limit_bytes=48 << 20),
        cost_estimate=pl.CostEstimate(flops=6 * steps * tile * width * out_width, bytes_accessed=6 * width * out_width, transcendentals=0),
    )(place, *args)


def put_kernel(n_pieces, place_ref, *refs):
    select_piece(pl.program_id(0), refs[:n_pieces], refs[-1])


def put_rows(place, pieces, block, prior=None):
    tile, width = pieces[0].shape
    steps = place.shape[0]
    args = [*pieces] + ([] if prior is None else [prior])
    return pl.pallas_call(
        functools.partial(put_kernel, len(pieces)),
        out_shape=jax.ShapeDtypeStruct((block, width), pieces[0].dtype),
        grid_spec=pltpu.PrefetchScalarGridSpec(
            num_scalar_prefetch=1, grid=(steps,),
            in_specs=piece_specs(pieces, tile) + ([] if prior is None else [pl.BlockSpec(memory_space=pl.ANY)]),
            out_specs=pl.BlockSpec((tile, width), lambda i, p: (p[i], 0))),
        input_output_aliases={} if prior is None else {1 + len(pieces): 0},
        compiler_params=pltpu.CompilerParams(dimension_semantics=("arbitrary",), vmem_limit_bytes=24 << 20),
        cost_estimate=pl.CostEstimate(flops=10 ** 9, bytes_accessed=4 * steps * tile * width, transcendentals=0),
    )(place, *args)


def normalize(hidden_f, gain):
    variance = jnp.mean(hidden_f * hidden_f, axis=-1, keepdims=True)
    return (hidden_f * lax.rsqrt(variance + 1e-6) * gain.astype(jnp.float32)).astype(jnp.bfloat16)


def rope_tables(positions):
    inv_freq = 1.0 / (1000000.0 ** (jnp.arange(0, HEAD_DIM, 2, dtype=jnp.float32) / HEAD_DIM))
    angles = positions.astype(jnp.float32)[:, None] * inv_freq[None, :]
    cos, sin = jnp.cos(angles), jnp.sin(angles)
    return jnp.concatenate([cos, cos], 1), jnp.concatenate([-sin, sin], 1)


def solution(mesh):
    tp_size = mesh.shape['tp']
    cp_size = mesh.shape['cp']
    swap_x = [(c, c ^ 2) for c in range(cp_size)]
    swap_core = [(c, c ^ 1) for c in range(cp_size)]
    to_later_chip = [(0, 2), (1, 3)]
    to_later_core = [(0, 1), (2, 3)]
    share_late_chip = [(2, 3), (3, 2)]

    def swap_tp(d):
        return [(t, t ^ d) for t in range(tp_size)]

    def local_step(x_in, positions, attn_gain, mlp_gain, w_query, b_query, w_key, b_key, w_value, b_value, w_out, w_gate, w_up, w_down):
        block, width = x_in.shape
        own = block // tp_size
        kv_width = w_key.shape[2]
        pair_width = kv_width // 2
        ffn_half = w_gate.shape[2] // 2
        col_half = width // 2
        t_idx = lax.axis_index('tp').astype(jnp.int32)
        c_idx = lax.axis_index('cp').astype(jnp.int32)
        x_idx = c_idx // 2
        core = c_idx % 2
        core_flag = core.reshape(1)

        def trade(w):
            return lax.ppermute(w, 'cp', swap_core)

        def after(value, *events):
            return lax.optimization_barrier((value,) + events)[0]

        def gather_out(part):
            return lax.all_gather(part, 'tp', axis=0, tiled=True)

        def out_part(layer):
            return lax.dynamic_slice(w_out, (layer, 0, core * col_half), (1, kv_width, col_half))[0]

        def down_part(layer):
            return lax.dynamic_slice(w_down, (layer, x_idx * ffn_half, core * col_half), (1, ffn_half, col_half))[0]

        def wide_part(layer, *events):
            w_gate_l, w_up_l = lax.optimization_barrier((w_gate, w_up) + events)[:2]
            cut = lambda w: lax.dynamic_slice(jnp.swapaxes(w, 1, 2), (layer, x_idx * ffn_half, 0), (1, ffn_half, width))[0]
            return jnp.where(core == 0, cut(w_gate_l), cut(w_up_l))

        def gather_stack(part):
            return lax.all_gather(part, 'tp', axis=0)

        def join_cols(mine, other):
            return jnp.where(core == 0, jnp.concatenate([mine, other], 1), jnp.concatenate([other, mine], 1))

        def places(k, chunks):
            return jnp.stack([(t_idx ^ d) * chunks + k for d in range(tp_size)])

        def spread_heads(attn):
            pieces = []
            for d in range(tp_size):
                piece = lax.dynamic_slice_in_dim(attn, (t_idx ^ d) * own, own, 0)
                pieces.append(lax.ppermute(piece, 'tp', swap_tp(d)) if d else piece)
            return pieces

        def collect_heads(groups):
            return jnp.concatenate([g[d] for d in range(tp_size) for g in groups], 1)

        def by_distance(gathered):
            return jnp.concatenate([lax.dynamic_slice_in_dim(gathered, (t_idx ^ d) * kv_width, kv_width, 0) for d in range(tp_size)], 0)

        def delta_of(distance):
            return (((c_idx ^ distance) - c_idx) * block).astype(jnp.int32)

        def attend(queries, packs, window, out_all, wide_all):
            near = jnp.stack([delta_of(0), delta_of(1)])
            far = jnp.stack([delta_of(2), delta_of(3)])
            nearby = [lax.ppermute(p, 'cp', to_later_core) for p in packs]
            remote = []
            for pack in packs:
                remote.append(lax.ppermute(pack, 'cp', to_later_chip))

            def local(g, first, count, held):
                return flash(held, (packs[g], nearby[g]), near, window, first, count, final=False, units=1.5)

            both = local(0, 0, 2, queries)
            held, both[1] = lax.optimization_barrier((queries, both[1]))
            third = local(1, 2, 1, held)
            held, third[1], far0 = lax.optimization_barrier((held, third[1], remote[0]))
            sources = (far0, lax.ppermute(far0, 'cp', share_late_chip))
            fourth = local(1, 3, 1, held)

            def finish(head, carry, start, held):
                return flash(held, sources if head < 2 else other, far, window, head, 1, carry=carry, start=start, units=2.0)

            held, fourth[1] = lax.optimization_barrier((held, fourth[1]))
            outs = [finish(0, both, 0, held)]
            far1, held, outs[0] = lax.optimization_barrier((remote[1], held, outs[0]))
            other = (far1, lax.ppermute(far1, 'cp', share_late_chip))
            sent = [spread_heads(outs[0])]
            outs.append(finish(1, both, 1, held))
            held, outs[1] = lax.optimization_barrier((held, outs[1]))
            sent.append(spread_heads(outs[1]))
            outs.append(finish(2, third, 0, held))
            held, outs[2], out_all, wide_all = lax.optimization_barrier((held, outs[2], out_all, wide_all))
            out_w = (out_all, trade(out_all))
            wide_w = (wide_all, trade(wide_all))
            sent.append(spread_heads(outs[2]))
            sent.append(spread_heads(finish(3, fourth, 0, held)))
            return collect_heads(sent), out_w, wide_w

        cos_tab, sin_tab = rope_tables(positions)
        residual = lax.dynamic_slice_in_dim(x_in, t_idx * own, own, 0).astype(jnp.float32)
        projections = ((w_query, w_key, w_value), (b_query, b_key, b_value))
        out_all = by_distance(gather_out(out_part(0)))
        chunks = 2
        piece = own // chunks
        fresh = qkv(0, True, jnp.arange(block // piece, dtype=jnp.int32), (x_in,), attn_gain, *projections, cos_tab, sin_tab, block, tile=piece)
        wide_all = gather_stack(wide_part(0, fresh[0]))
        down_all = gather_stack(after(down_part(0), fresh[0]))
        caches = []
        for layer in range(2):
            window = block * cp_size if layer == 0 else WINDOW
            queries, packs = fresh[0], fresh[1:]
            heads_all, out_w, wide_w = attend(queries, packs, window, out_all, wide_all)
            proj = join_cols(*(jnp.dot(heads_all, w, preferred_element_type=jnp.float32) for w in out_w))
            mid = (residual + proj).astype(jnp.bfloat16)
            h_mid = normalize(mid.astype(jnp.float32), mlp_gain[layer])
            guests = [lax.ppermute(h_mid[k * piece:(k + 1) * piece], 'cp', swap_x) for k in range(chunks)]
            h_mid, down_all = lax.optimization_barrier((h_mid, down_all))
            down_w = (down_all, trade(down_all))
            if layer == 0:
                out_all = by_distance(gather_out(after(out_part(1), h_mid)))
                down_all = gather_stack(after(down_part(1), h_mid))
            mine = mlp(core_flag, h_mid, *wide_w, *down_w, residual=mid)
            guests[0], mine = lax.optimization_barrier((guests[0], mine))
            guest_out = mlp(core_flag, guests[0], *wide_w, *down_w)
            back = [lax.ppermute(guest_out, 'cp', swap_x)]
            guests[1], guest_out = lax.optimization_barrier((guests[1], guest_out))
            guest_last = mlp(core_flag, guests[1], *wide_w, *down_w)
            back.append(lax.ppermute(guest_last, 'cp', swap_x))
            back[0], guest_last = lax.optimization_barrier((back[0], guest_last))
            heads = lambda at: jnp.concatenate([p[:, at:at + pair_width] for p in packs], 1).reshape(block, -1, HEAD_DIM)
            held = [heads(0), heads(pair_width)]
            caches += held
            rest, result, last = [], None, back[1]
            if layer == 0:
                wide_next, last = lax.optimization_barrier((wide_part(1, guest_last), last))
            for k in range(chunks):
                from_guest = back[0] if k == 0 else last
                hidden = (mine[k * piece:(k + 1) * piece] + from_guest.astype(jnp.float32)).astype(jnp.bfloat16)
                rest.append(hidden.astype(jnp.float32))
                rows = normalize(rest[k], attn_gain[1]) if layer == 0 else hidden
                by_y = lax.ppermute(rows, 'tp', swap_tp(1))
                by_z = lax.ppermute(rows, 'tp', swap_tp(2))
                if k == 0:
                    by_y, by_z, last = lax.optimization_barrier((by_y, by_z, last))
                elif layer == 0:
                    by_y, by_z, result[0] = lax.optimization_barrier((by_y, by_z, result[0]))
                else:
                    by_y, by_z, result = lax.optimization_barrier((by_y, by_z, result))
                half = piece // 2
                pieces = (rows, by_y, by_z, lax.ppermute(by_y[:half], 'tp', swap_tp(2)), lax.ppermute(by_z[half:], 'tp', swap_tp(1)))
                if layer == 0:
                    result = list(qkv(1, False, places(k, chunks), pieces, attn_gain, *projections, cos_tab, sin_tab, block, prior=result, tile=piece))
                else:
                    result = put_rows(places(k, chunks), pieces, block, result)
            if layer == 0:
                fresh = result
                residual = jnp.concatenate(rest, 0)
                wide_all = gather_stack(after(wide_next, fresh[0], down_all))
        return result, caches[0], caches[1], caches[2], caches[3]

    weight_col = P(None, None, 'tp')
    bias_col = P(None, 'tp')
    weight_row = P(None, 'tp', None)
    replicated = P(None, None)
    cache_spec = P('cp', 'tp', None)
    in_specs = (P('cp', None), P('cp'), replicated, replicated, weight_col, bias_col, weight_col, bias_col, weight_col, bias_col, weight_row, weight_col, weight_col, weight_row)
    out_specs = (P('cp', None), cache_spec, cache_spec, cache_spec, cache_spec)
    return jax.shard_map(local_step, mesh=mesh, in_specs=in_specs, out_specs=out_specs, check_vma=False)
```

profile of v0, /device:TPU:0, one launch (start us, length us, event | category | flops | bytes accessed | tf_op | source)
XLA Modules:
  0.0 874.4 jit_solution(1027142280001863891)
XLA Ops:
  14.9 22.4 %shard_map.173 = (bf16[2048,512]{1,0:T(8,128)(2,1)S(1)}, bf16[2048,512]{1,0:T(8,128)(2,1)}, bf16[2048,512]{1,0:T(8,128)(2,1)}) custom-call(s32[8]{0:T(128)S(1)} %iota.8.place_ref, bf16[2048,2048]{1,0:T(8,128)(2,1)} %refs_0_.1, bf16[2,2048]{1,0:T(2,128)(2,1)S(1)} %copy-done.20, bf16[2,2048,512]{2,1,0:T(8,128)(2,1)} %refs_6_.5, bf16[2,2048,512]{2,1,0:T(8,128)(2,1)} %refs_7_.5, ...), custom_call_target="tpu_custom_call" | custom-call | flops 12884901888 | bytes 6291456 | tf_op jit(solution)/shard_map/pallas_call | solution.py:276
  58.7 15.7 %shard_map.174 = (f32[256,2048]{1,0:T(8,128)S(1)}, f32[2,8,2048]{2,1,0:T(8,128)S(1)}) custom-call(s32[2]{0:T(128)S(1)} %pad_add_fusion.1.deltas, bf16[2048,512]{1,0:T(8,128)(2,1)S(1)} %copy-done.27, bf16[2048,512]{1,0:T(8,128)(2,1)} %get-tuple-element.94.refs_0_.refs_1_, bf16[2048,512]{1,0:T(8,128)(2,1)} %get-tuple-element.94.refs_0_.refs_1_, ...), custom_call_target="tpu_custom_call" | custom-call | flops 6442450944 | bytes 4194304 | tf_op jit(solution)/shard_map/pallas_call | solution.py:142
  75.7 9.1 %shard_map.175 = (f32[128,2048]{1,0:T(8,128)S(1)}, f32[1,8,2048]{2,1,0:T(8,128)S(1)}) custom-call(s32[2]{0:T(128)S(1)} %pad_add_fusion.1.deltas, bf16[2048,512]{1,0:T(8,128)(2,1)S(1)} %copy-done.27, bf16[2048,512]{1,0:T(8,128)(2,1)S(1)} %copy-done.11, bf16[2048,512]{1,0:T(8,128)(2,1)S(1)} %copy-done.11, ...), custom_call_target="tpu_custom_call" | custom-call | flops 3221225472 | bytes 2097152 | tf_op jit(solution)/shard_map/pallas_call | solution.py:142
  85.8 11.8 %collective-permute-done.3.refs_0_.refs_1_ = bf16[2048,512]{1,0:T(8,128)(2,1)} collective-permute-done((bf16[2048,512]{1,0:T(8,128)(2,1)}, bf16[2048,512]{1,0:T(8,128)(2,1)}, u32[]{:S(2)}, u32[]{:S(2)}) %collective-permute-start.3) | collective-permute-done | bytes 2097184 | tf_op jit(solution)/shard_map/ppermute | solution.py:398
  99.7 9.5 %collective-permute-start = (bf16[2048,512]{1,0:T(8,128)(2,1)S(1)}, bf16[2048,512]{1,0:T(8,128)(2,1)}, u32[]{:S(2)}, u32[]{:S(2)}) collective-permute-start(bf16[2048,512]{1,0:T(8,128)(2,1)S(1)} %copy-done.11), channel_id=1, source_target_pairs={{0,2},{1,3},{4,6},{5,7},{8,10},{9,11},{12,14},{13,15}} | collective-permute-start | bytes 6291464 | tf_op jit(solution)/shard_map/ppermute | solution.py:398
  111.5 8.9 %shard_map.176 = (f32[128,2048]{1,0:T(8,128)S(1)}, f32[1,8,2048]{2,1,0:T(8,128)S(1)}) custom-call(s32[2]{0:T(128)S(1)} %pad_add_fusion.1.deltas, bf16[2048,512]{1,0:T(8,128)(2,1)S(1)} %copy-done.28, bf16[2048,512]{1,0:T(8,128)(2,1)S(1)} %copy-done.11, bf16[2048,512]{1,0:T(8,128)(2,1)S(1)} %copy-done.11, ...), custom_call_target="tpu_custom_call" | custom-call | flops 3221225472 | bytes 2097152 | tf_op jit(solution)/shard_map/pallas_call | solution.py:142
  124.8 28.1 %collective-permute-done.refs_0_.refs_1_ = bf16[2048,512]{1,0:T(8,128)(2,1)} collective-permute-done((bf16[2048,512]{1,0:T(8,128)(2,1)S(1)}, bf16[2048,512]{1,0:T(8,128)(2,1)}, u32[]{:S(2)}, u32[]{:S(2)}) %collective-permute-start) | collective-permute-done | bytes 2097184 | tf_op jit(solution)/shard_map/ppermute | solution.py:398
  181.2 12.0 %shard_map.180 = bf16[2048,128]{1,0:T(8,128)(2,1)S(1)} custom-call(s32[2]{0:T(128)S(1)} %pad_add_fusion.2.deltas, bf16[2048,512]{1,0:T(8,128)(2,1)S(1)} %copy-done.30, bf16[2048,512]{1,0:T(8,128)(2,1)} %collective-permute-done.refs_0_.refs_1_, bf16[2048,512]{1,0:T(8,128)(2,1)} %collective-permute-done.refs_0_.refs_1_, ...), custom_call_target="tpu_custom_call" | custom-call | flops 4294967296 | bytes 2097152 | tf_op jit(solution)/shard_map/pallas_call | solution.py:142
  210.4 7.9 collective-permute-done.12
  244.0 9.5 %all-gather.17.cloned.1.call-done = bf16[2752,1024]{1,0:T(8,128)(2,1)} async-done(((bf16[688,1024]{1,0:T(8,128)(2,1)}), bf16[2752,1024]{1,0:T(8,128)(2,1)}) %all-gather.17.cloned.1.call-update) | async-done | bytes 5636112 | tf_op jit(solution)/shard_map/all_gather | solution.py:368
  256.7 17.9 %collective-permute-start.19 = (bf16[256,2048]{1,0:T(8,128)(2,1)}, bf16[256,2048]{1,0:T(8,128)(2,1)S(1)}, u32[]{:S(2)}, u32[]{:S(2)}) collective-permute-start(bf16[256,2048]{1,0:T(8,128)(2,1)} %get-tuple-element.210), channel_id=1, source_target_pairs={{0,2},{1,3},{2,0},{3,1},{4,6},{5,7},{6,4},{7,5},{8,10},{9,11},{10,... | collective-permute-start | bytes 3145736 | tf_op jit(solution)/shard_map/ppermute | solution.py:446
  274.8 31.3 %shard_map.181 = f32[512,2048]{1,0:T(8,128)} custom-call(s32[1]{0:T(128)} %bitcast.13.first_ref, bf16[512,2048]{1,0:T(8,128)(2,1)} %fusion.2.h_ref, bf16[4,688,2048]{2,1,0:T(8,128)(2,1)} %all-gather.11.cloned.1.call-done.a_ref, bf16[4,688,2048]{2,1,0:T(8,128)(2,1)} %collective-permute-done.20.b_ref, bf16[4,688,1024]{2,1,0:T(8,128)(2,1)} %bitcast.57, ...), custom_call_target="tpu_custom_call" | custom-call | flops 17314086912 | bytes 33816576 | tf_op jit(solution)/shard_map/pallas_call | solution.py:196
  307.0 17.6 %shard_map.182 = bf16[256,2048]{1,0:T(8,128)(2,1)} custom-call(s32[1]{0:T(128)} %bitcast.13.first_ref, bf16[256,2048]{1,0:T(8,128)(2,1)} %copy-done.55, bf16[4,688,2048]{2,1,0:T(8,128)(2,1)} %all-gather.11.cloned.1.call-done.a_ref, bf16[4,688,2048]{2,1,0:T(8,128)(2,1)} %collective-permute-done.20.b_ref, bf16[4,688,1024]{2,1,0:T(8,128)(2,1)} %bitcast.58, ...), custom_call_target="tpu_custom_call" | custom-call | flops 8657043456 | bytes 33816576 | tf_op jit(solution)/shard_map/pallas_call | solution.py:196
  324.6 7.5 collective-permute-start.22
  333.2 18.8 %shard_map.183 = bf16[256,2048]{1,0:T(8,128)(2,1)} custom-call(s32[1]{0:T(128)} %bitcast.13.first_ref, bf16[256,2048]{1,0:T(8,128)(2,1)} %copy-done.53, bf16[4,688,2048]{2,1,0:T(8,128)(2,1)} %all-gather.11.cloned.1.call-done.a_ref, bf16[4,688,2048]{2,1,0:T(8,128)(2,1)} %collective-permute-done.20.b_ref, bf16[4,688,1024]{2,1,0:T(8,128)(2,1)} %bitcast.59, ...), custom_call_target="tpu_custom_call" | custom-call | flops 8657043456 | bytes 33816576 | tf_op jit(solution)/shard_map/pallas_call | solution.py:196
  365.8 12.6 %collective-permute-done.26 = bf16[256,2048]{1,0:T(8,128)(2,1)} collective-permute-done((bf16[256,2048]{1,0:T(8,128)(2,1)}, bf16[256,2048]{1,0:T(8,128)(2,1)}, u32[]{:S(2)}, u32[]{:S(2)}) %collective-permute-start.26) | collective-permute-done | bytes 1048608 | tf_op jit(solution)/shard_map/ppermute | solution.py:458
  378.4 25.4 %collective-permute-done.24.refs_1_ = bf16[256,2048]{1,0:T(8,128)(2,1)S(1)} collective-permute-done((bf16[256,2048]{1,0:T(8,128)(2,1)S(1)}, bf16[256,2048]{1,0:T(8,128)(2,1)S(1)}, u32[]{:S(2)}, u32[]{:S(2)}) %collective-permute-start.24) | collective-permute-done | bytes 1048608 | tf_op jit(solution)/shard_map/ppermute | solution.py:471
  425.7 13.2 %shard_map.184 = (bf16[2048,512]{1,0:T(8,128)(2,1)}, bf16[2048,512]{1,0:T(8,128)(2,1)}, bf16[2048,512]{1,0:T(8,128)(2,1)}) custom-call(s32[4]{0:T(128)S(1)} %pad_add_fusion.3.place_ref, bf16[256,2048]{1,0:T(8,128)(2,1)S(1)} %copy-done.14, bf16[256,2048]{1,0:T(8,128)(2,1)S(1)} %copy-done.19, bf16[256,2048]{1,0:T(8,128)(2,1)} %collective-permute-done.25.refs_2_, ...), custom_call_target="tpu_custom_call" | custom-call | flops 6442450944 | bytes 6291456 | tf_op jit(solution)/shard_map/pallas_call | solution.py:276
  448.5 8.5 collective-permute-done.31.refs_3_
  459.2 13.2 %shard_map.185 = (bf16[2048,512]{1,0:T(8,128)(2,1)}, bf16[2048,512]{1,0:T(8,128)(2,1)}, bf16[2048,512]{1,0:T(8,128)(2,1)}) custom-call(s32[4]{0:T(128)S(1)} %pad_add_fusion.place_ref, bf16[256,2048]{1,0:T(8,128)(2,1)S(1)} %multiply_convert_fusion.refs_0_, ...), custom_call_target="tpu_custom_call", output_to_operand_aliasing={{0}: (15, {}), {1}: (16, {}), {2}: (17, {})} | custom-call | flops 6442450944 | bytes 6291456 | tf_op jit(solution)/shard_map/pallas_call | solution.py:276
  481.8 16.3 %shard_map.186 = (f32[256,2048]{1,0:T(8,128)S(1)}, f32[2,8,2048]{2,1,0:T(8,128)S(1)}) custom-call(s32[2]{0:T(128)S(1)} %pad_add_fusion.1.deltas, bf16[2048,512]{1,0:T(8,128)(2,1)S(1)} %copy-done.8, bf16[2048,512]{1,0:T(8,128)(2,1)} %get-tuple-element.140.refs_0_.refs_1_, bf16[2048,512]{1,0:T(8,128)(2,1)} %get-tuple-element.140.refs_0_.refs_1_, ...), custom_call_target="tpu_custom_call" | custom-call | flops 6442450944 | bytes 4194304 | tf_op jit(solution)/shard_map/pallas_call | solution.py:142
  499.5 8.9 %shard_map.187 = (f32[128,2048]{1,0:T(8,128)S(1)}, f32[1,8,2048]{2,1,0:T(8,128)S(1)}) custom-call(s32[2]{0:T(128)S(1)} %pad_add_fusion.1.deltas, bf16[2048,512]{1,0:T(8,128)(2,1)S(1)} %copy-done.8, bf16[2048,512]{1,0:T(8,128)(2,1)S(1)} %copy-done, bf16[2048,512]{1,0:T(8,128)(2,1)S(1)} %copy-done, bf16[2048,512]{1,0:T(8,128)(2,1)} %copy-done.60, ...), custom_call_target="tpu_custom_call" | custom-call | flops 3221225472 | bytes 2097152 | tf_op jit(solution)/shard_map/pallas_call | solution.py:142
  509.4 11.1 %collective-permute-done.36.refs_0_.refs_1_ = bf16[2048,512]{1,0:T(8,128)(2,1)S(1)} collective-permute-done((bf16[2048,512]{1,0:T(8,128)(2,1)}, bf16[2048,512]{1,0:T(8,128)(2,1)S(1)}, u32[]{:S(2)}, u32[]{:S(2)}) %collective-permute-start.36) | collective-permute-done | bytes 2097184 | tf_op jit(solution)/shard_map/ppermute | solution.py:398
  521.5 15.6 %collective-permute-start.33 = (bf16[2048,512]{1,0:T(8,128)(2,1)S(1)}, bf16[2048,512]{1,0:T(8,128)(2,1)}, u32[]{:S(2)}, u32[]{:S(2)}) collective-permute-start(bf16[2048,512]{1,0:T(8,128)(2,1)S(1)} %copy-done), channel_id=1, source_target_pairs={{0,2},{1,3},{4,6},{5,7},{8,10},{9,11},{12,14},{13,15}} | collective-permute-start | bytes 6291464 | tf_op jit(solution)/shard_map/ppermute | solution.py:398
  537.1 8.7 shard_map.188
  551.5 29.3 %collective-permute-done.33.refs_0_.refs_1_ = bf16[2048,512]{1,0:T(8,128)(2,1)} collective-permute-done((bf16[2048,512]{1,0:T(8,128)(2,1)S(1)}, bf16[2048,512]{1,0:T(8,128)(2,1)}, u32[]{:S(2)}, u32[]{:S(2)}) %collective-permute-start.33) | collective-permute-done | bytes 2097184 | tf_op jit(solution)/shard_map/ppermute | solution.py:398
  603.3 8.7 shard_map.192
  663.5 34.5 %collective-permute-start.52 = (bf16[256,2048]{1,0:T(8,128)(2,1)}, bf16[256,2048]{1,0:T(8,128)(2,1)}, u32[]{:S(2)}, u32[]{:S(2)}) collective-permute-start(bf16[256,2048]{1,0:T(8,128)(2,1)} %get-tuple-element.208), channel_id=1, source_target_pairs={{0,2},{1,3},{2,0},{3,1},{4,6},{5,7},{6,4},{7,5},{8,10},{9,11},{10,... | collective-permute-start | bytes 3145736 | tf_op jit(solution)/shard_map/ppermute | solution.py:446
  700.5 30.1 %shard_map.193 = f32[512,2048]{1,0:T(8,128)} custom-call(s32[1]{0:T(128)} %bitcast.13.first_ref, bf16[512,2048]{1,0:T(8,128)(2,1)} %copy-done.46, bf16[4,688,2048]{2,1,0:T(8,128)(2,1)} %bitcast.47, bf16[4,688,2048]{2,1,0:T(8,128)(2,1)} %collective-permute-done.53.b_ref, bf16[4,688,1024]{2,1,0:T(8,128)(2,1)} %bitcast.50, bf16[4,688,1024]{2,1,0:T(8,128)(2,1)} %copy-done.41, ...), custom_call_target="tpu_custom_call" | custom-call | flops 17314086912 | bytes 33816576 | tf_op jit(solution)/shard_map/pallas_call | solution.py:196
  730.6 18.0 %shard_map.194 = bf16[256,2048]{1,0:T(8,128)(2,1)} custom-call(s32[1]{0:T(128)} %bitcast.13.first_ref, bf16[256,2048]{1,0:T(8,128)(2,1)} %collective-permute-done.52.h_ref, bf16[4,688,2048]{2,1,0:T(8,128)(2,1)} %bitcast.48, bf16[4,688,2048]{2,1,0:T(8,128)(2,1)} %collective-permute-done.53.b_ref, bf16[4,688,1024]{2,1,0:T(8,128)(2,1)} %bitcast.51, ...), custom_call_target="tpu_custom_call" | custom-call | flops 8657043456 | bytes 33816576 | tf_op jit(solution)/shard_map/pallas_call | solution.py:196
  758.3 18.2 %shard_map.195 = bf16[256,2048]{1,0:T(8,128)(2,1)} custom-call(s32[1]{0:T(128)} %bitcast.13.first_ref, bf16[256,2048]{1,0:T(8,128)(2,1)} %copy-done.54, bf16[4,688,2048]{2,1,0:T(8,128)(2,1)} %bitcast.49, bf16[4,688,2048]{2,1,0:T(8,128)(2,1)} %collective-permute-done.53.b_ref, bf16[4,688,1024]{2,1,0:T(8,128)(2,1)} %bitcast.52, bf16[4,688,1024]{2,1,0:T(8,128)(2,1)} %copy-done.41), custom_call_target="tpu_custom_call" | custom-call | flops 8657043456 | bytes 33816576 | tf_op jit(solution)/shard_map/pallas_call | solution.py:196
  817.2 26.8 %collective-permute-done.62.refs_3_ = bf16[128,2048]{1,0:T(8,128)(2,1)S(1)} collective-permute-done((bf16[128,2048]{1,0:T(8,128)(2,1)S(1)}, bf16[128,2048]{1,0:T(8,128)(2,1)S(1)}, u32[]{:S(2)}, u32[]{:S(2)}) %collective-permute-start.62) | collective-permute-done | bytes 524320 | tf_op jit(solution)/shard_map/ppermute | solution.py:480
  (363 shorter events, 331.6 us)
Async XLA Ops:
  7.2 163.4 %all-gather.15.cloned.1.call-start = ((), (), s32[]{:S(2)}) async-start(), calls=%async_computation.2 | async-start | bytes 5242880 | tf_op jit(solution)/shard_map/all_gather | solution.py:354
  10.3 165.2 %all-gather.11.cloned.1.call-start = ((), (), s32[]{:S(2)}) async-start(), calls=%async_computation | async-start | bytes 14090240 | tf_op jit(solution)/shard_map/all_gather | solution.py:368
  44.1 209.3 %all-gather.17.cloned.1.call-start = ((), (), s32[]{:S(2)}) async-start(), calls=%async_computation.3 | async-start | bytes 7045120 | tf_op jit(solution)/shard_map/all_gather | solution.py:368
  48.4 27.3 %collective-permute-start.2 = (bf16[2048,512]{1,0:T(8,128)(2,1)S(1)}, bf16[2048,512]{1,0:T(8,128)(2,1)}, u32[]{:S(2)}, u32[]{:S(2)}) collective-permute-start(bf16[2048,512]{1,0:T(8,128)(2,1)S(1)} %copy-done.11), channel_id=1, source_target_pairs={{0,1},{2,3},{4,5},{6,7},{8,9},{10,11},{12,13},{14,15}} | collective-permute-start | bytes 6291464 | tf_op jit(solution)/shard_map/ppermute | solution.py:395
  51.0 46.7 %collective-permute-start.3 = (bf16[2048,512]{1,0:T(8,128)(2,1)}, bf16[2048,512]{1,0:T(8,128)(2,1)}, u32[]{:S(2)}, u32[]{:S(2)}) collective-permute-start(bf16[2048,512]{1,0:T(8,128)(2,1)} %get-tuple-element.94.refs_0_.refs_1_), channel_id=1, source_target_pairs={{0,2},{1,3},{4,6},{5,7},{8,10},{9,11},{12,14},{13,15}} | collective-permute-start | bytes 6291464 | tf_op jit(solution)/shard_map/ppermute | solution.py:398
  99.7 53.2 %collective-permute-start = (bf16[2048,512]{1,0:T(8,128)(2,1)S(1)}, bf16[2048,512]{1,0:T(8,128)(2,1)}, u32[]{:S(2)}, u32[]{:S(2)}) collective-permute-start(bf16[2048,512]{1,0:T(8,128)(2,1)S(1)} %copy-done.11), channel_id=1, source_target_pairs={{0,2},{1,3},{4,6},{5,7},{8,10},{9,11},{12,14},{13,15}} | collective-permute-start | bytes 6291464 | tf_op jit(solution)/shard_map/ppermute | solution.py:398
  158.5 313.9 %all-gather.19.cloned.1.call-start = ((), (), s32[]{:S(2)}) async-start(), calls=%async_computation.4 | async-start | bytes 7045120 | tf_op jit(solution)/shard_map/all_gather | solution.py:368
  175.5 61.8 %collective-permute-start.18 = (bf16[2048,1024]{1,0:T(8,128)(2,1)}, bf16[2048,1024]{1,0:T(8,128)(2,1)S(1)}, u32[]{:S(2)}, u32[]{:S(2)}) collective-permute-start(bf16[2048,1024]{1,0:T(8,128)(2,1)} %pad_maximum_fusion), channel_id=1, source_target_pairs={{0,1},{1,0},{2,3},{3,2},{4,5},{5,4},{6,7},{7,6},{8,9},{9,8},{10,11... | collective-permute-start | bytes 12582920 | tf_op jit(solution)/shard_map/ppermute | solution.py:348
  177.8 30.4 %collective-permute-start.10 = (bf16[512,128]{1,0:T(8,128)(2,1)S(1)}, bf16[512,128]{1,0:T(8,128)(2,1)S(1)}, u32[]{:S(2)}, u32[]{:S(2)}) collective-permute-start(bf16[512,128]{1,0:T(8,128)(2,1)S(1)} %get-tuple-element.240), channel_id=1, source_target_pairs={{0,8},{4,12},{8,0},{12,4},{1,9},{5,13},{9,1},{13,5},{2,10},{6,14},... | collective-permute-start | bytes 393224 | tf_op jit(solution)/shard_map/ppermute | solution.py:380
  179.4 29.3 %collective-permute-start.11 = (bf16[512,128]{1,0:T(8,128)(2,1)S(1)}, bf16[512,128]{1,0:T(8,128)(2,1)S(1)}, u32[]{:S(2)}, u32[]{:S(2)}) collective-permute-start(bf16[512,128]{1,0:T(8,128)(2,1)S(1)} %get-tuple-element.236), channel_id=1, source_target_pairs={{0,8},{4,12},{8,0},{12,4},{1,9},{5,13},{9,1},{13,5},{2,10},{6,14},... | collective-permute-start | bytes 393224 | tf_op jit(solution)/shard_map/ppermute | solution.py:380
  227.8 46.9 %collective-permute-start.20 = (bf16[4,688,2048]{2,1,0:T(8,128)(2,1)}, bf16[4,688,2048]{2,1,0:T(8,128)(2,1)}, u32[]{:S(2)}, u32[]{:S(2)}) collective-permute-start(bf16[4,688,2048]{2,1,0:T(8,128)(2,1)} %all-gather.11.cloned.1.call-done.a_ref), channel_id=1, source_target_pairs={{0,1},{1,0},{2,3},{3,2},{4,5},{5,4},{6,7},{7,6},{8,9},{9,8},{10,11... | collective-permute-start | bytes 33816584 | tf_op jit(solution)/shard_map/ppermute | solution.py:348
  253.5 329.5 %all-gather.13.cloned.1.call-start = ((), (), s32[]{:S(2)}) async-start(), calls=%async_computation.1 | async-start | bytes 5242880 | tf_op jit(solution)/shard_map/all_gather | solution.py:354
  256.7 49.4 %collective-permute-start.19 = (bf16[256,2048]{1,0:T(8,128)(2,1)}, bf16[256,2048]{1,0:T(8,128)(2,1)S(1)}, u32[]{:S(2)}, u32[]{:S(2)}) collective-permute-start(bf16[256,2048]{1,0:T(8,128)(2,1)} %get-tuple-element.210), channel_id=1, source_target_pairs={{0,2},{1,3},{2,0},{3,1},{4,6},{5,7},{6,4},{7,5},{8,10},{9,11},{10,... | collective-permute-start | bytes 3145736 | tf_op jit(solution)/shard_map/ppermute | solution.py:446
  274.6 57.6 %collective-permute-start.23 = (bf16[256,2048]{1,0:T(8,128)(2,1)}, bf16[256,2048]{1,0:T(8,128)(2,1)S(1)}, u32[]{:S(2)}, u32[]{:S(2)}) collective-permute-start(bf16[256,2048]{1,0:T(8,128)(2,1)} %get-tuple-element.209), channel_id=1, source_target_pairs={{0,2},{1,3},{2,0},{3,1},{4,6},{5,7},{6,4},{7,5},{8,10},{9,11},{10,... | collective-permute-start | bytes 3145736 | tf_op jit(solution)/shard_map/ppermute | solution.py:446
  274.7 321.9 %all-gather.21.cloned.1.call-start = ((), (), s32[]{:S(2)}) async-start(), calls=%async_computation.5 | async-start | bytes 14090240 | tf_op jit(solution)/shard_map/all_gather | solution.py:368
  324.6 31.7 %collective-permute-start.22 = (bf16[256,2048]{1,0:T(8,128)(2,1)}, bf16[256,2048]{1,0:T(8,128)(2,1)S(1)}, u32[]{:S(2)}, u32[]{:S(2)}) collective-permute-start(bf16[256,2048]{1,0:T(8,128)(2,1)} %shard_map.182), channel_id=1, source_target_pairs={{0,2},{1,3},{2,0},{3,1},{4,6},{5,7},{6,4},{7,5},{8,10},{9,11},{10,... | collective-permute-start | bytes 3145736 | tf_op jit(solution)/shard_map/ppermute | solution.py:455
  358.0 45.8 %collective-permute-start.24 = (bf16[256,2048]{1,0:T(8,128)(2,1)S(1)}, bf16[256,2048]{1,0:T(8,128)(2,1)S(1)}, u32[]{:S(2)}, u32[]{:S(2)}) collective-permute-start(bf16[256,2048]{1,0:T(8,128)(2,1)S(1)} %multiply_convert_fusion.1.refs_0_), channel_id=1, source_target_pairs={{0,4},{4,0},{8,12},{12,8},{1,5},{5,1},{9,13},{13,9},{2,6},{6,2},{1... | collective-permute-start | bytes 3145736 | tf_op jit(solution)/shard_map/ppermute | solution.py:471
  359.9 44.1 %collective-permute-start.25 = (bf16[256,2048]{1,0:T(8,128)(2,1)S(1)}, bf16[256,2048]{1,0:T(8,128)(2,1)}, u32[]{:S(2)}, u32[]{:S(2)}) collective-permute-start(bf16[256,2048]{1,0:T(8,128)(2,1)S(1)} %multiply_convert_fusion.1.refs_0_), channel_id=1, source_target_pairs={{0,8},{4,12},{8,0},{12,4},{1,9},{5,13},{9,1},{13,5},{2,10},{6,14},... | collective-permute-start | bytes 3145736 | tf_op jit(solution)/shard_map/ppermute | solution.py:472
  412.4 31.3 %collective-permute-start.27 = (bf16[256,2048]{1,0:T(8,128)(2,1)S(1)}, bf16[256,2048]{1,0:T(8,128)(2,1)S(1)}, u32[]{:S(2)}, u32[]{:S(2)}) collective-permute-start(bf16[256,2048]{1,0:T(8,128)(2,1)S(1)} %multiply_convert_fusion.refs_0_), channel_id=1, source_target_pairs={{0,4},{4,0},{8,12},{12,8},{1,5},{5,1},{9,13},{13,9},{2,6},{6,2},{1... | collective-permute-start | bytes 3145736 | tf_op jit(solution)/shard_map/ppermute | solution.py:471
  413.7 30.0 %collective-permute-start.28 = (bf16[256,2048]{1,0:T(8,128)(2,1)S(1)}, bf16[256,2048]{1,0:T(8,128)(2,1)}, u32[]{:S(2)}, u32[]{:S(2)}) collective-permute-start(bf16[256,2048]{1,0:T(8,128)(2,1)S(1)} %multiply_convert_fusion.refs_0_), channel_id=1, source_target_pairs={{0,8},{4,12},{8,0},{12,4},{1,9},{5,13},{9,1},{13,5},{2,10},{6,14},... | collective-permute-start | bytes 3145736 | tf_op jit(solution)/shard_map/ppermute | solution.py:472
  475.4 45.1 %collective-permute-start.36 = (bf16[2048,512]{1,0:T(8,128)(2,1)}, bf16[2048,512]{1,0:T(8,128)(2,1)S(1)}, u32[]{:S(2)}, u32[]{:S(2)}) collective-permute-start(bf16[2048,512]{1,0:T(8,128)(2,1)} %get-tuple-element.140.refs_0_.refs_1_), channel_id=1, source_target_pairs={{0,2},{1,3},{4,6},{5,7},{8,10},{9,11},{12,14},{13,15}} | collective-permute-start | bytes 6291464 | tf_op jit(solution)/shard_map/ppermute | solution.py:398
  521.5 59.3 %collective-permute-start.33 = (bf16[2048,512]{1,0:T(8,128)(2,1)S(1)}, bf16[2048,512]{1,0:T(8,128)(2,1)}, u32[]{:S(2)}, u32[]{:S(2)}) collective-permute-start(bf16[2048,512]{1,0:T(8,128)(2,1)S(1)} %copy-done), channel_id=1, source_target_pairs={{0,2},{1,3},{4,6},{5,7},{8,10},{9,11},{12,14},{13,15}} | collective-permute-start | bytes 6291464 | tf_op jit(solution)/shard_map/ppermute | solution.py:398
  596.6 49.1 %collective-permute-start.51 = (bf16[2048,1024]{1,0:T(8,128)(2,1)}, bf16[2048,1024]{1,0:T(8,128)(2,1)}, u32[]{:S(2)}, u32[]{:S(2)}) collective-permute-start(bf16[2048,1024]{1,0:T(8,128)(2,1)} %pad_maximum_fusion.1), channel_id=1, source_target_pairs={{0,1},{1,0},{2,3},{3,2},{4,5},{5,4},{6,7},{7,6},{8,9},{9,8},{10,11... | collective-permute-start | bytes 12582920 | tf_op jit(solution)/shard_map/ppermute | solution.py:348
  596.7 103.8 %collective-permute-start.53 = (bf16[4,688,2048]{2,1,0:T(8,128)(2,1)}, bf16[4,688,2048]{2,1,0:T(8,128)(2,1)}, u32[]{:S(2)}, u32[]{:S(2)}) collective-permute-start(bf16[4,688,2048]{2,1,0:T(8,128)(2,1)} %bitcast.46), channel_id=1, source_target_pairs={{0,1},{1,0},{2,3},{3,2},{4,5},{5,4},{6,7},{7,6},{8,9},{9,8},{10,11... | collective-permute-start | bytes 33816584 | tf_op jit(solution)/shard_map/ppermute | solution.py:348
  661.5 36.5 %collective-permute-start.54 = (bf16[4,688,1024]{2,1,0:T(8,128)(2,1)S(1)}, bf16[4,688,1024]{2,1,0:T(8,128)(2,1)S(1)}, u32[]{:S(2)}, u32[]{:S(2)}) collective-permute-start(bf16[4,688,1024]{2,1,0:T(8,128)(2,1)S(1)} %bitcast.55), channel_id=1, source_target_pairs={{0,1},{1,0},{2,3},{3,2},{4,5},{5,4},{6,7},{7,6},{8,9},{9,8},{10,11... | collective-permute-start | bytes 16908296 | tf_op jit(solution)/shard_map/ppermute | solution.py:348
  663.5 67.1 %collective-permute-start.52 = (bf16[256,2048]{1,0:T(8,128)(2,1)}, bf16[256,2048]{1,0:T(8,128)(2,1)}, u32[]{:S(2)}, u32[]{:S(2)}) collective-permute-start(bf16[256,2048]{1,0:T(8,128)(2,1)} %get-tuple-element.208), channel_id=1, source_target_pairs={{0,2},{1,3},{2,0},{3,1},{4,6},{5,7},{6,4},{7,5},{8,10},{9,11},{10,... | collective-permute-start | bytes 3145736 | tf_op jit(solution)/shard_map/ppermute | solution.py:446
  697.9 59.3 %collective-permute-start.56 = (bf16[256,2048]{1,0:T(8,128)(2,1)}, bf16[256,2048]{1,0:T(8,128)(2,1)S(1)}, u32[]{:S(2)}, u32[]{:S(2)}) collective-permute-start(bf16[256,2048]{1,0:T(8,128)(2,1)} %get-tuple-element.207), channel_id=1, source_target_pairs={{0,2},{1,3},{2,0},{3,1},{4,6},{5,7},{6,4},{7,5},{8,10},{9,11},{10,... | collective-permute-start | bytes 3145736 | tf_op jit(solution)/shard_map/ppermute | solution.py:446
  748.6 31.4 %collective-permute-start.55 = (bf16[256,2048]{1,0:T(8,128)(2,1)}, bf16[256,2048]{1,0:T(8,128)(2,1)}, u32[]{:S(2)}, u32[]{:S(2)}) collective-permute-start(bf16[256,2048]{1,0:T(8,128)(2,1)} %shard_map.194), channel_id=1, source_target_pairs={{0,2},{1,3},{2,0},{3,1},{4,6},{5,7},{6,4},{7,5},{8,10},{9,11},{10,... | collective-permute-start | bytes 3145736 | tf_op jit(solution)/shard_map/ppermute | solution.py:455
  808.5 40.0 %collective-permute-start.60 = (bf16[256,2048]{1,0:T(8,128)(2,1)S(1)}, bf16[256,2048]{1,0:T(8,128)(2,1)S(1)}, u32[]{:S(2)}, u32[]{:S(2)}) collective-permute-start(bf16[256,2048]{1,0:T(8,128)(2,1)S(1)} %add_convert_fusion.refs_0_), channel_id=1, source_target_pairs={{0,4},{4,0},{8,12},{12,8},{1,5},{5,1},{9,13},{13,9},{2,6},{6,2},{1... | collective-permute-start | bytes 3145736 | tf_op jit(solution)/shard_map/ppermute | solution.py:471
  809.9 38.6 %collective-permute-start.61 = (bf16[256,2048]{1,0:T(8,128)(2,1)S(1)}, bf16[256,2048]{1,0:T(8,128)(2,1)S(1)}, u32[]{:S(2)}, u32[]{:S(2)}) collective-permute-start(bf16[256,2048]{1,0:T(8,128)(2,1)S(1)} %add_convert_fusion.refs_0_), channel_id=1, source_target_pairs={{0,8},{4,12},{8,0},{12,4},{1,9},{5,13},{9,1},{13,5},{2,10},{6,14},... | collective-permute-start | bytes 3145736 | tf_op jit(solution)/shard_map/ppermute | solution.py:472
  812.7 31.3 %collective-permute-start.62 = (bf16[128,2048]{1,0:T(8,128)(2,1)S(1)}, bf16[128,2048]{1,0:T(8,128)(2,1)S(1)}, u32[]{:S(2)}, u32[]{:S(2)}) collective-permute-start(bf16[128,2048]{1,0:T(8,128)(2,1)S(1)} %slice.97), channel_id=1, source_target_pairs={{0,8},{4,12},{8,0},{12,4},{1,9},{5,13},{9,1},{13,5},{2,10},{6,14},... | collective-permute-start | bytes 1572872 | tf_op jit(solution)/shard_map/ppermute | solution.py:480
  815.3 28.7 %collective-permute-start.63 = (bf16[128,2048]{1,0:T(8,128)(2,1)S(1)}, bf16[128,2048]{1,0:T(8,128)(2,1)S(1)}, u32[]{:S(2)}, u32[]{:S(2)}) collective-permute-start(bf16[128,2048]{1,0:T(8,128)(2,1)S(1)} %slice.98), channel_id=1, source_target_pairs={{0,4},{4,0},{8,12},{12,8},{1,5},{5,1},{9,13},{13,9},{2,6},{6,2},{1... | collective-permute-start | bytes 1572872 | tf_op jit(solution)/shard_map/ppermute | solution.py:480
  (104 other events, 1014.8 us)
Sparse Core Ops, SparseCore 0:
  10.4 51.6 all-gather.14
  63.9 107.7 all-gather.10
  173.4 79.9 all-gather.16
  255.1 75.9 all-gather.18
  332.8 70.2 all-gather.12
  472.6 107.4 all-gather.20
where the time goes:
time: 882 us; the launch traced here: 874 us
  Pallas kernels  303 us (34%)
  waiting for transfers between devices  242 us (27%)
  starting transfers between devices  167 us (19%)
  local copies, waits for them, and re-layouts  82.8 us (9%)
  other arithmetic  48.3 us (5%)
  between operations  15.9 us (2%)
  matrix products  15 us (2%)
    pallas_call x6, Pallas kernels, mlp(): pl.pallas_call(functools.partial(mlp_kernel, min(tile, rows)), out_shape=...  134 us
    pallas_call x14, Pallas kernels, flash(): pl.pallas_call(functools.partial(flash_kernel, n_src, window, bq, bk, cha...  111 us
    ppermute x4, waiting for transfers between devices, attend(): remote.append(lax.ppermute(pack, 'cp', to_later_chip))  80.4 us
    ppermute x4, starting transfers between devices, local_step(): lax.ppermute(h_mid[k * piece:(k + 1) * piece], 'cp', swap_x)  52.4 us
    pallas_call x3, Pallas kernels, qkv(): pl.pallas_call(functools.partial(qkv_kernel, layer, norm, len(pieces)), o...  48.7 us
    ppermute x24, waiting for transfers between devices, spread_heads(): pieces.append(lax.ppermute(piece, 'tp', swap_tp(d)) if d else piece)  46.2 us
    ppermute x4, waiting for transfers between devices, local_step(): lax.ppermute(by_y[:half], 'tp', swap_tp(2))  40.8 us
    unnamed x150, local copies, waits for them, and re-layouts  36.1 us
  transfers between devices with their start and end apart: 72, of which 33 were waited for; matrix products, arithmetic and copies ran while one was open for 12% of the time, Pallas kernels for 34%

commit v1 on v0

--- a/solution.py
+++ b/solution.py
@@ -48,24 +48,31 @@
     cw = bq // chains
     kc, ec = 256, 32
     parts = bk // kc
-
-    def step(k_ref, vt, delta, j, masked):
+    assert bq == bk and cw == kc and window % bk == 0
+
+    def step(k_ref, vt, j, edge):
         off = pl.multiple_of(j * bk, bk)
+
+        def span(c):
+            if edge == 'causal':
+                return range(c + 1)
+            return range(c, parts) if edge == 'window' else range(parts)
 
         def scores(c, r):
             kb = k_ref[pl.ds(off + r * kc, kc), :]
             s = lax.dot_general(kb, q_ref[c * cw:(c + 1) * cw, :], (((1,), (1,)), ((), ())), preferred_element_type=jnp.float32)
-            if masked:
-                rel = lax.broadcasted_iota(jnp.int32, (kc, cw), 0) - lax.broadcasted_iota(jnp.int32, (kc, cw), 1) + (delta + off + r * kc - t0 - c * cw)
-                s = jnp.where((rel <= 0) & (rel > -window), s, NEG)
+            if edge and r == c:
+                key_at, query_at = (lax.broadcasted_iota(jnp.int32, (kc, cw), axis) for axis in range(2))
+                s = jnp.where(key_at <= query_at if edge == 'causal' else key_at > query_at, s, NEG)
             s_bufs[c % 2][r * kc:(r + 1) * kc, :] = s
             return jnp.max(s.reshape(kc // 8, 8, cw), axis=0)
 
         def weigh(c, alpha):
             sl = slice(c * cw, (c + 1) * cw)
-            acc[:, sl] = acc[:, sl] * alpha + jnp.dot(vt[:, pl.ds(off, bk)], p_bufs[c % 2][...], preferred_element_type=jnp.float32)
-
-        top = functools.reduce(jnp.maximum, [scores(0, r) for r in range(parts)])
+            lo, hi = span(c)[0] * kc, (span(c)[-1] + 1) * kc
+            acc[:, sl] = acc[:, sl] * alpha + jnp.dot(vt[:, pl.ds(off + lo, hi - lo)], p_bufs[c % 2][lo:hi, :], preferred_element_type=jnp.float32)
+
+        top = functools.reduce(jnp.maximum, [scores(0, r) for r in span(0)])
         pending = None
         for c in range(chains):
             sl = slice(c * cw, (c + 1) * cw)
@@ -73,16 +80,19 @@
             m_new = jnp.maximum(m_prev, jnp.max(top, axis=0, keepdims=True))
             alpha = jnp.exp2((m_prev - m_new) * EXP_SCALE)
             stat[0:1, sl] = m_new
+            following = list(span(c + 1)) if c + 1 < chains else []
             tops, total = [], None
-            for r in range(parts):
-                if c + 1 < chains:
-                    tops.append(scores(c + 1, r))
-                for e in range(r * kc, (r + 1) * kc, ec):
-                    p = jnp.exp2((s_bufs[c % 2][e:e + ec, :] - m_new) * EXP_SCALE)
-                    p_bufs[c % 2][e:e + ec, :] = p.astype(jnp.bfloat16)
-                    part = jnp.sum(p.reshape(ec // 8, 8, cw), axis=0)
-                    total = part if total is None else total + part
-                if r == 0 and pending is not None:
+            for n in range(parts):
+                if n < len(following):
+                    tops.append(scores(c + 1, following[n]))
+                if n < len(span(c)):
+                    r = span(c)[n]
+                    for e in range(r * kc, (r + 1) * kc, ec):
+                        p = jnp.exp2((s_bufs[c % 2][e:e + ec, :] - m_new) * EXP_SCALE)
+                        p_bufs[c % 2][e:e + ec, :] = p.astype(jnp.bfloat16)
+                        part = jnp.sum(p.reshape(ec // 8, 8, cw), axis=0)
+                        total = part if total is None else total + part
+                if n == 0 and pending is not None:
                     weigh(*pending)
             stat[1:2, sl] = stat[1:2, sl] * alpha + jnp.sum(total, axis=0, keepdims=True)
             pending = (c, alpha)
@@ -100,16 +110,16 @@
         lo_full = jnp.minimum(lo_full, hi_any)
         hi_full = jnp.maximum(hi_full, lo_full)
 
-        def body(masked):
+        def body(edge):
             def f(j, _):
-                step(kv[2 * n], vts[n], delta, j, masked)
+                step(kv[2 * n], vts[n], j, edge)
                 return 0
 
             return f
 
-        lax.fori_loop(lo_any, lo_full, body(True), 0)
-        lax.fori_loop(lo_full, hi_full, body(False), 0)
-        lax.fori_loop(hi_full, hi_any, body(True), 0)
+        lax.fori_loop(lo_any, lo_full, body('window'), 0)
+        lax.fori_loop(lo_full, hi_full, body(None), 0)
+        lax.fori_loop(hi_full, hi_any, body('causal'), 0)
     if final:
         o_ref[...] = (acc[...] * (1.0 / stat[1:2, :])).T.astype(o_ref.dtype)
     else:
@@ -459,8 +469,9 @@
             back[0], guest_last = lax.optimization_barrier((back[0], guest_last))
             heads = lambda at: jnp.concatenate([p[:, at:at + pair_width] for p in packs], 1).reshape(block, -1, HEAD_DIM)
             held = [heads(0), heads(pair_width)]
+            rest, result, last = [], None, back[1]
+            held[0], held[1], last = lax.optimization_barrier((held[0], held[1], last))
             caches += held
-            rest, result, last = [], None, back[1]
             if layer == 0:
                 wide_next, last = lax.optimization_barrier((wide_part(1, guest_last), last))
             for k in range(chunks):

time: 882 us -> 871 us (0.988)
  Pallas kernels: 303 us -> 278 us
  local copies, waits for them, and re-layouts: 82.8 us -> 94.3 us
    pallas_call x14, Pallas kernels: 111 us -> 88.1 us  [flash(): pl.pallas_call(functools.partial(flash_kernel, n_src, window, bq, bk, cha...]
    unnamed x150 -> x154, local copies, waits for them, and re-layouts: 36.1 us -> 46.6 us
    ppermute x4, waiting for transfers between devices: 80.4 us -> 90.9 us  [attend(): remote.append(lax.ppermute(pack, 'cp', to_later_chip))]
  transfers between devices with their start and end apart: 72 -> 72, of which waited for: 33 -> 34; matrix products, arithmetic and copies ran while one was open for 12% -> 13% of each run, Pallas kernels for 34% -> 32%
where the time goes in v1:
time: 871 us; the launch traced here: 863 us
  Pallas kernels  278 us (32%)
  waiting for transfers between devices  248 us (28%)
  starting transfers between devices  161 us (18%)
  local copies, waits for them, and re-layouts  94.3 us (11%)
  other arithmetic  47.3 us (5%)
  matrix products  18.9 us (2%)
  between operations  15.4 us (2%)
    pallas_call x6, Pallas kernels, mlp(): pl.pallas_call(functools.partial(mlp_kernel, min(tile, rows)), out_shape=...  133 us
    ppermute x4, waiting for transfers between devices, attend(): remote.append(lax.ppermute(pack, 'cp', to_later_chip))  90.9 us
    pallas_call x14, Pallas kernels, flash(): pl.pallas_call(functools.partial(flash_kernel, n_src, window, bq, bk, cha...  88.1 us
    ppermute x4, starting transfers between devices, local_step(): lax.ppermute(h_mid[k * piece:(k + 1) * piece], 'cp', swap_x)  60 us
    ppermute x4, waiting for transfers between devices, local_step(): lax.ppermute(by_y[:half], 'tp', swap_tp(2))  49 us
    pallas_call x3, Pallas kernels, qkv(): pl.pallas_call(functools.partial(qkv_kernel, layer, norm, len(pieces)), o...  48.7 us
    unnamed x154, local copies, waits for them, and re-layouts  46.6 us
    ppermute x24, waiting for transfers between devices, spread_heads(): pieces.append(lax.ppermute(piece, 'tp', swap_tp(d)) if d else piece)  45.6 us
  transfers between devices with their start and end apart: 72, of which 34 were waited for; matrix products, arithmetic and copies ran while one was open for 13% of the time, Pallas kernels for 32%

profile of v1, /device:TPU:0, one launch (start us, length us, event | category | flops | bytes accessed | tf_op | source)
XLA Modules:
  0.0 863.2 jit_solution(13944415403562365778)
XLA Ops:
  14.9 22.3 %shard_map.173 = (bf16[2048,512]{1,0:T(8,128)(2,1)S(1)}, bf16[2048,512]{1,0:T(8,128)(2,1)}, bf16[2048,512]{1,0:T(8,128)(2,1)}) custom-call(s32[8]{0:T(128)S(1)} %iota.8.place_ref, bf16[2048,2048]{1,0:T(8,128)(2,1)} %refs_0_.1, bf16[2,2048]{1,0:T(2,128)(2,1)S(1)} %copy-done.18, bf16[2,2048,512]{2,1,0:T(8,128)(2,1)} %refs_6_.5, bf16[2,2048,512]{2,1,0:T(8,128)(2,1)} %refs_7_.5, ...), custom_call_target="tpu_custom_call" | custom-call | flops 12884901888 | bytes 6291456 | tf_op jit(solution)/shard_map/pallas_call | solution.py:286
  51.1 6.1 collective-permute-start.3
  58.8 12.0 %shard_map.174 = (f32[256,2048]{1,0:T(8,128)S(1)}, f32[2,8,2048]{2,1,0:T(8,128)S(1)}) custom-call(s32[2]{0:T(128)S(1)} %pad_add_fusion.1.deltas, bf16[2048,512]{1,0:T(8,128)(2,1)S(1)} %copy-done.25, bf16[2048,512]{1,0:T(8,128)(2,1)} %get-tuple-element.100.refs_0_.refs_1_, bf16[2048,512]{1,0:T(8,128)(2,1)} %get-tuple-element.100.refs_0_.refs_1_, ...), custom_call_target="tpu_custom_call" | custom-call | flops 6442450944 | bytes 4194304 | tf_op jit(solution)/shard_map/pallas_call | solution.py:152
  72.1 7.6 shard_map.175
  80.7 16.9 %collective-permute-done.3.refs_0_.refs_1_ = bf16[2048,512]{1,0:T(8,128)(2,1)} collective-permute-done((bf16[2048,512]{1,0:T(8,128)(2,1)}, bf16[2048,512]{1,0:T(8,128)(2,1)}, u32[]{:S(2)}, u32[]{:S(2)}) %collective-permute-start.3) | collective-permute-done | bytes 2097184 | tf_op jit(solution)/shard_map/ppermute | solution.py:408
  107.0 7.2 shard_map.176
  118.7 30.8 %collective-permute-done.refs_0_.refs_1_ = bf16[2048,512]{1,0:T(8,128)(2,1)} collective-permute-done((bf16[2048,512]{1,0:T(8,128)(2,1)S(1)}, bf16[2048,512]{1,0:T(8,128)(2,1)}, u32[]{:S(2)}, u32[]{:S(2)}) %collective-permute-start) | collective-permute-done | bytes 2097184 | tf_op jit(solution)/shard_map/ppermute | solution.py:408
  254.7 29.6 %collective-permute-start.19 = (bf16[256,2048]{1,0:T(8,128)(2,1)S(1)}, bf16[256,2048]{1,0:T(8,128)(2,1)S(1)}, u32[]{:S(2)}, u32[]{:S(2)}) collective-permute-start(bf16[256,2048]{1,0:T(8,128)(2,1)S(1)} %get-tuple-element.222), channel_id=1, source_target_pairs={{0,2},{1,3},{2,0},{3,1},{4,6},{5,7},{6,4},{7,5},{8,10},{9,11},{10,... | collective-permute-start | bytes 3145736 | tf_op jit(solution)/shard_map/ppermute | solution.py:456
  284.4 31.1 %shard_map.181 = f32[512,2048]{1,0:T(8,128)} custom-call(s32[1]{0:T(128)} %bitcast.13.first_ref, bf16[512,2048]{1,0:T(8,128)(2,1)} %fusion.2.h_ref, bf16[4,688,2048]{2,1,0:T(8,128)(2,1)} %all-gather.11.cloned.1.call-done.a_ref, bf16[4,688,2048]{2,1,0:T(8,128)(2,1)} %collective-permute-done.20.b_ref, bf16[4,688,1024]{2,1,0:T(8,128)(2,1)} %bitcast.57, ...), custom_call_target="tpu_custom_call" | custom-call | flops 17314086912 | bytes 33816576 | tf_op jit(solution)/shard_map/pallas_call | solution.py:206
  316.5 17.6 %shard_map.182 = bf16[256,2048]{1,0:T(8,128)(2,1)} custom-call(s32[1]{0:T(128)} %bitcast.13.first_ref, bf16[256,2048]{1,0:T(8,128)(2,1)} %copy-done.56, bf16[4,688,2048]{2,1,0:T(8,128)(2,1)} %all-gather.11.cloned.1.call-done.a_ref, bf16[4,688,2048]{2,1,0:T(8,128)(2,1)} %collective-permute-done.20.b_ref, bf16[4,688,1024]{2,1,0:T(8,128)(2,1)} %bitcast.58, ...), custom_call_target="tpu_custom_call" | custom-call | flops 8657043456 | bytes 33816576 | tf_op jit(solution)/shard_map/pallas_call | solution.py:206
  340.1 18.4 %shard_map.183 = bf16[256,2048]{1,0:T(8,128)(2,1)} custom-call(s32[1]{0:T(128)} %bitcast.13.first_ref, bf16[256,2048]{1,0:T(8,128)(2,1)} %copy-done.54, bf16[4,688,2048]{2,1,0:T(8,128)(2,1)} %all-gather.11.cloned.1.call-done.a_ref, bf16[4,688,2048]{2,1,0:T(8,128)(2,1)} %collective-permute-done.20.b_ref, bf16[4,688,1024]{2,1,0:T(8,128)(2,1)} %bitcast.59, ...), custom_call_target="tpu_custom_call" | custom-call | flops 8657043456 | bytes 33816576 | tf_op jit(solution)/shard_map/pallas_call | solution.py:206
  385.5 24.5 %collective-permute-done.24.refs_1_ = bf16[256,2048]{1,0:T(8,128)(2,1)S(1)} collective-permute-done((bf16[256,2048]{1,0:T(8,128)(2,1)S(1)}, bf16[256,2048]{1,0:T(8,128)(2,1)S(1)}, u32[]{:S(2)}, u32[]{:S(2)}) %collective-permute-start.24) | collective-permute-done | bytes 1048608 | tf_op jit(solution)/shard_map/ppermute | solution.py:482
  432.6 13.2 %shard_map.184 = (bf16[2048,512]{1,0:T(8,128)(2,1)}, bf16[2048,512]{1,0:T(8,128)(2,1)}, bf16[2048,512]{1,0:T(8,128)(2,1)}) custom-call(s32[4]{0:T(128)S(1)} %pad_add_fusion.3.place_ref, bf16[256,2048]{1,0:T(8,128)(2,1)S(1)} %copy-done.7, bf16[256,2048]{1,0:T(8,128)(2,1)S(1)} %copy-done.17, bf16[256,2048]{1,0:T(8,128)(2,1)} %collective-permute-done.25.refs_2_, ...), custom_call_target="tpu_custom_call" | custom-call | flops 6442450944 | bytes 6291456 | tf_op jit(solution)/shard_map/pallas_call | solution.py:286
  451.5 7.2 collective-permute-done.31.refs_3_
  460.6 13.2 %shard_map.185 = (bf16[2048,512]{1,0:T(8,128)(2,1)}, bf16[2048,512]{1,0:T(8,128)(2,1)}, bf16[2048,512]{1,0:T(8,128)(2,1)}) custom-call(s32[4]{0:T(128)S(1)} %pad_add_fusion.place_ref, bf16[256,2048]{1,0:T(8,128)(2,1)S(1)} %multiply_convert_fusion.refs_0_, ...), custom_call_target="tpu_custom_call", output_to_operand_aliasing={{0}: (15, {}), {1}: (16, {}), {2}: (17, {})} | custom-call | flops 6442450944 | bytes 6291456 | tf_op jit(solution)/shard_map/pallas_call | solution.py:286
  482.6 12.6 %shard_map.186 = (f32[256,2048]{1,0:T(8,128)S(1)}, f32[2,8,2048]{2,1,0:T(8,128)S(1)}) custom-call(s32[2]{0:T(128)S(1)} %pad_add_fusion.1.deltas, bf16[2048,512]{1,0:T(8,128)(2,1)S(1)} %copy-done.2, bf16[2048,512]{1,0:T(8,128)(2,1)} %get-tuple-element.147.refs_0_.refs_1_, bf16[2048,512]{1,0:T(8,128)(2,1)} %get-tuple-element.147.refs_0_.refs_1_, ...), custom_call_target="tpu_custom_call" | custom-call | flops 6442450944 | bytes 4194304 | tf_op jit(solution)/shard_map/pallas_call | solution.py:152
  497.8 7.0 shard_map.187
  505.8 12.2 %collective-permute-done.36.refs_0_.refs_1_ = bf16[2048,512]{1,0:T(8,128)(2,1)S(1)} collective-permute-done((bf16[2048,512]{1,0:T(8,128)(2,1)}, bf16[2048,512]{1,0:T(8,128)(2,1)S(1)}, u32[]{:S(2)}, u32[]{:S(2)}) %collective-permute-start.36) | collective-permute-done | bytes 2097184 | tf_op jit(solution)/shard_map/ppermute | solution.py:408
  518.9 14.1 %collective-permute-start.33 = (bf16[2048,512]{1,0:T(8,128)(2,1)S(1)}, bf16[2048,512]{1,0:T(8,128)(2,1)}, u32[]{:S(2)}, u32[]{:S(2)}) collective-permute-start(bf16[2048,512]{1,0:T(8,128)(2,1)S(1)} %copy-done), channel_id=1, source_target_pairs={{0,2},{1,3},{4,6},{5,7},{8,10},{9,11},{12,14},{13,15}} | collective-permute-start | bytes 6291464 | tf_op jit(solution)/shard_map/ppermute | solution.py:408
  533.0 7.1 shard_map.188
  545.8 30.9 %collective-permute-done.33.refs_0_.refs_1_ = bf16[2048,512]{1,0:T(8,128)(2,1)} collective-permute-done((bf16[2048,512]{1,0:T(8,128)(2,1)S(1)}, bf16[2048,512]{1,0:T(8,128)(2,1)}, u32[]{:S(2)}, u32[]{:S(2)}) %collective-permute-start.33) | collective-permute-done | bytes 2097184 | tf_op jit(solution)/shard_map/ppermute | solution.py:408
  601.1 9.0 %shard_map.192 = bf16[2048,128]{1,0:T(8,128)(2,1)S(1)} custom-call(s32[2]{0:T(128)S(1)} %pad_add_fusion.2.deltas, bf16[2048,512]{1,0:T(8,128)(2,1)S(1)} %copy-done.4, bf16[2048,512]{1,0:T(8,128)(2,1)} %collective-permute-done.33.refs_0_.refs_1_, bf16[2048,512]{1,0:T(8,128)(2,1)} %collective-permute-done.33.refs_0_.refs_1_, ...), custom_call_target="tpu_custom_call" | custom-call | flops 4294967296 | bytes 2097152 | tf_op jit(solution)/shard_map/pallas_call | solution.py:152
  643.3 6.6 fusion.25
  649.9 7.0 fusion.3
  661.1 30.3 %collective-permute-start.52 = (bf16[256,2048]{1,0:T(8,128)(2,1)}, bf16[256,2048]{1,0:T(8,128)(2,1)}, u32[]{:S(2)}, u32[]{:S(2)}) collective-permute-start(bf16[256,2048]{1,0:T(8,128)(2,1)} %get-tuple-element.216), channel_id=1, source_target_pairs={{0,2},{1,3},{2,0},{3,1},{4,6},{5,7},{6,4},{7,5},{8,10},{9,11},{10,... | collective-permute-start | bytes 3145736 | tf_op jit(solution)/shard_map/ppermute | solution.py:456
  693.9 30.1 %shard_map.193 = f32[512,2048]{1,0:T(8,128)} custom-call(s32[1]{0:T(128)} %bitcast.13.first_ref, bf16[512,2048]{1,0:T(8,128)(2,1)} %copy-done.46, bf16[4,688,2048]{2,1,0:T(8,128)(2,1)} %bitcast.47, bf16[4,688,2048]{2,1,0:T(8,128)(2,1)} %collective-permute-done.53.b_ref, bf16[4,688,1024]{2,1,0:T(8,128)(2,1)} %bitcast.50, bf16[4,688,1024]{2,1,0:T(8,128)(2,1)} %copy-done.40, ...), custom_call_target="tpu_custom_call" | custom-call | flops 17314086912 | bytes 33816576 | tf_op jit(solution)/shard_map/pallas_call | solution.py:206
  724.0 17.9 %shard_map.194 = bf16[256,2048]{1,0:T(8,128)(2,1)} custom-call(s32[1]{0:T(128)} %bitcast.13.first_ref, bf16[256,2048]{1,0:T(8,128)(2,1)} %collective-permute-done.52.h_ref, bf16[4,688,2048]{2,1,0:T(8,128)(2,1)} %bitcast.48, bf16[4,688,2048]{2,1,0:T(8,128)(2,1)} %collective-permute-done.53.b_ref, bf16[4,688,1024]{2,1,0:T(8,128)(2,1)} %bitcast.51, ...), custom_call_target="tpu_custom_call" | custom-call | flops 8657043456 | bytes 33816576 | tf_op jit(solution)/shard_map/pallas_call | solution.py:206
  741.9 7.2 collective-permute-start.55
  751.6 18.2 %shard_map.195 = bf16[256,2048]{1,0:T(8,128)(2,1)} custom-call(s32[1]{0:T(128)} %bitcast.13.first_ref, bf16[256,2048]{1,0:T(8,128)(2,1)} %copy-done.55, bf16[4,688,2048]{2,1,0:T(8,128)(2,1)} %bitcast.49, bf16[4,688,2048]{2,1,0:T(8,128)(2,1)} %collective-permute-done.53.b_ref, bf16[4,688,1024]{2,1,0:T(8,128)(2,1)} %bitcast.52, bf16[4,688,1024]{2,1,0:T(8,128)(2,1)} %copy-done.40), custom_call_target="tpu_custom_call" | custom-call | flops 8657043456 | bytes 33816576 | tf_op jit(solution)/shard_map/pallas_call | solution.py:206
  784.0 11.3 %collective-permute-done.59 = bf16[256,2048]{1,0:T(8,128)(2,1)} collective-permute-done((bf16[256,2048]{1,0:T(8,128)(2,1)}, bf16[256,2048]{1,0:T(8,128)(2,1)}, u32[]{:S(2)}, u32[]{:S(2)}) %collective-permute-start.59) | collective-permute-done | bytes 1048608 | tf_op jit(solution)/shard_map/ppermute | solution.py:468
  808.2 29.1 %collective-permute-done.62.refs_3_ = bf16[128,2048]{1,0:T(8,128)(2,1)S(1)} collective-permute-done((bf16[128,2048]{1,0:T(8,128)(2,1)S(1)}, bf16[128,2048]{1,0:T(8,128)(2,1)S(1)}, u32[]{:S(2)}, u32[]{:S(2)}) %collective-permute-start.62) | collective-permute-done | bytes 524320 | tf_op jit(solution)/shard_map/ppermute | solution.py:491
  844.2 8.5 collective-permute-done.64.refs_3_
  (367 shorter events, 330.9 us)
Async XLA Ops:
  7.2 160.5 %all-gather.15.cloned.1.call-start = ((), (), s32[]{:S(2)}) async-start(), calls=%async_computation.2 | async-start | bytes 5242880 | tf_op jit(solution)/shard_map/all_gather | solution.py:364
  10.3 162.3 %all-gather.11.cloned.1.call-start = ((), (), s32[]{:S(2)}) async-start(), calls=%async_computation | async-start | bytes 14090240 | tf_op jit(solution)/shard_map/all_gather | solution.py:378
  44.1 207.0 %all-gather.17.cloned.1.call-start = ((), (), s32[]{:S(2)}) async-start(), calls=%async_computation.3 | async-start | bytes 7045120 | tf_op jit(solution)/shard_map/all_gather | solution.py:378
  51.1 46.6 %collective-permute-start.3 = (bf16[2048,512]{1,0:T(8,128)(2,1)}, bf16[2048,512]{1,0:T(8,128)(2,1)}, u32[]{:S(2)}, u32[]{:S(2)}) collective-permute-start(bf16[2048,512]{1,0:T(8,128)(2,1)} %get-tuple-element.100.refs_0_.refs_1_), channel_id=1, source_target_pairs={{0,2},{1,3},{4,6},{5,7},{8,10},{9,11},{12,14},{13,15}} | collective-permute-start | bytes 6291464 | tf_op jit(solution)/shard_map/ppermute | solution.py:408
  99.7 49.8 %collective-permute-start = (bf16[2048,512]{1,0:T(8,128)(2,1)S(1)}, bf16[2048,512]{1,0:T(8,128)(2,1)}, u32[]{:S(2)}, u32[]{:S(2)}) collective-permute-start(bf16[2048,512]{1,0:T(8,128)(2,1)S(1)} %copy-done.5), channel_id=1, source_target_pairs={{0,2},{1,3},{4,6},{5,7},{8,10},{9,11},{12,14},{13,15}} | collective-permute-start | bytes 6291464 | tf_op jit(solution)/shard_map/ppermute | solution.py:408
  155.1 318.7 %all-gather.19.cloned.1.call-start = ((), (), s32[]{:S(2)}) async-start(), calls=%async_computation.4 | async-start | bytes 7045120 | tf_op jit(solution)/shard_map/all_gather | solution.py:378
  172.6 63.4 %collective-permute-start.18 = (bf16[2048,1024]{1,0:T(8,128)(2,1)}, bf16[2048,1024]{1,0:T(8,128)(2,1)}, u32[]{:S(2)}, u32[]{:S(2)}) collective-permute-start(bf16[2048,1024]{1,0:T(8,128)(2,1)} %pad_maximum_fusion), channel_id=1, source_target_pairs={{0,1},{1,0},{2,3},{3,2},{4,5},{5,4},{6,7},{7,6},{8,9},{9,8},{10,11... | collective-permute-start | bytes 12582920 | tf_op jit(solution)/shard_map/ppermute | solution.py:358
  172.6 111.8 %collective-permute-start.20 = (bf16[4,688,2048]{2,1,0:T(8,128)(2,1)}, bf16[4,688,2048]{2,1,0:T(8,128)(2,1)}, u32[]{:S(2)}, u32[]{:S(2)}) collective-permute-start(bf16[4,688,2048]{2,1,0:T(8,128)(2,1)} %all-gather.11.cloned.1.call-done.a_ref), channel_id=1, source_target_pairs={{0,1},{1,0},{2,3},{3,2},{4,5},{5,4},{6,7},{7,6},{8,9},{9,8},{10,11... | collective-permute-start | bytes 33816584 | tf_op jit(solution)/shard_map/ppermute | solution.py:358
  251.1 33.3 %collective-permute-start.21 = (bf16[4,688,1024]{2,1,0:T(8,128)(2,1)}, bf16[4,688,1024]{2,1,0:T(8,128)(2,1)}, u32[]{:S(2)}, u32[]{:S(2)}) collective-permute-start(bf16[4,688,1024]{2,1,0:T(8,128)(2,1)} %bitcast.56), channel_id=1, source_target_pairs={{0,1},{1,0},{2,3},{3,2},{4,5},{5,4},{6,7},{7,6},{8,9},{9,8},{10,11... | collective-permute-start | bytes 16908296 | tf_op jit(solution)/shard_map/ppermute | solution.py:358
  251.1 327.6 %all-gather.13.cloned.1.call-start = ((), (), s32[]{:S(2)}) async-start(), calls=%async_computation.1 | async-start | bytes 5242880 | tf_op jit(solution)/shard_map/all_gather | solution.py:364
  254.7 60.8 %collective-permute-start.19 = (bf16[256,2048]{1,0:T(8,128)(2,1)S(1)}, bf16[256,2048]{1,0:T(8,128)(2,1)S(1)}, u32[]{:S(2)}, u32[]{:S(2)}) collective-permute-start(bf16[256,2048]{1,0:T(8,128)(2,1)S(1)} %get-tuple-element.222), channel_id=1, source_target_pairs={{0,2},{1,3},{2,0},{3,1},{4,6},{5,7},{6,4},{7,5},{8,10},{9,11},{10,... | collective-permute-start | bytes 3145736 | tf_op jit(solution)/shard_map/ppermute | solution.py:456
  284.4 54.8 %collective-permute-start.23 = (bf16[256,2048]{1,0:T(8,128)(2,1)}, bf16[256,2048]{1,0:T(8,128)(2,1)S(1)}, u32[]{:S(2)}, u32[]{:S(2)}) collective-permute-start(bf16[256,2048]{1,0:T(8,128)(2,1)} %get-tuple-element.221), channel_id=1, source_target_pairs={{0,2},{1,3},{2,0},{3,1},{4,6},{5,7},{6,4},{7,5},{8,10},{9,11},{10,... | collective-permute-start | bytes 3145736 | tf_op jit(solution)/shard_map/ppermute | solution.py:456
  334.1 29.2 %collective-permute-start.22 = (bf16[256,2048]{1,0:T(8,128)(2,1)}, bf16[256,2048]{1,0:T(8,128)(2,1)S(1)}, u32[]{:S(2)}, u32[]{:S(2)}) collective-permute-start(bf16[256,2048]{1,0:T(8,128)(2,1)} %shard_map.182), channel_id=1, source_target_pairs={{0,2},{1,3},{2,0},{3,1},{4,6},{5,7},{6,4},{7,5},{8,10},{9,11},{10,... | collective-permute-start | bytes 3145736 | tf_op jit(solution)/shard_map/ppermute | solution.py:465
  339.1 253.9 %all-gather.21.cloned.1.call-start = ((), (), s32[]{:S(2)}) async-start(), calls=%async_computation.5 | async-start | bytes 14090240 | tf_op jit(solution)/shard_map/all_gather | solution.py:378
  358.5 27.0 %collective-permute-start.26 = (bf16[256,2048]{1,0:T(8,128)(2,1)}, bf16[256,2048]{1,0:T(8,128)(2,1)}, u32[]{:S(2)}, u32[]{:S(2)}) collective-permute-start(bf16[256,2048]{1,0:T(8,128)(2,1)} %shard_map.183), channel_id=1, source_target_pairs={{0,2},{1,3},{2,0},{3,1},{4,6},{5,7},{6,4},{7,5},{8,10},{9,11},{10,... | collective-permute-start | bytes 3145736 | tf_op jit(solution)/shard_map/ppermute | solution.py:468
  363.9 46.1 %collective-permute-start.24 = (bf16[256,2048]{1,0:T(8,128)(2,1)S(1)}, bf16[256,2048]{1,0:T(8,128)(2,1)S(1)}, u32[]{:S(2)}, u32[]{:S(2)}) collective-permute-start(bf16[256,2048]{1,0:T(8,128)(2,1)S(1)} %multiply_convert_fusion.1.refs_0_), channel_id=1, source_target_pairs={{0,4},{4,0},{8,12},{12,8},{1,5},{5,1},{9,13},{13,9},{2,6},{6,2},{1... | collective-permute-start | bytes 3145736 | tf_op jit(solution)/shard_map/ppermute | solution.py:482
  364.6 46.4 %collective-permute-start.25 = (bf16[256,2048]{1,0:T(8,128)(2,1)S(1)}, bf16[256,2048]{1,0:T(8,128)(2,1)}, u32[]{:S(2)}, u32[]{:S(2)}) collective-permute-start(bf16[256,2048]{1,0:T(8,128)(2,1)S(1)} %multiply_convert_fusion.1.refs_0_), channel_id=1, source_target_pairs={{0,8},{4,12},{8,0},{12,4},{1,9},{5,13},{9,1},{13,5},{2,10},{6,14},... | collective-permute-start | bytes 3145736 | tf_op jit(solution)/shard_map/ppermute | solution.py:483
  420.2 27.8 %collective-permute-start.27 = (bf16[256,2048]{1,0:T(8,128)(2,1)S(1)}, bf16[256,2048]{1,0:T(8,128)(2,1)S(1)}, u32[]{:S(2)}, u32[]{:S(2)}) collective-permute-start(bf16[256,2048]{1,0:T(8,128)(2,1)S(1)} %multiply_convert_fusion.refs_0_), channel_id=1, source_target_pairs={{0,4},{4,0},{8,12},{12,8},{1,5},{5,1},{9,13},{13,9},{2,6},{6,2},{1... | collective-permute-start | bytes 3145736 | tf_op jit(solution)/shard_map/ppermute | solution.py:482
  420.7 27.3 %collective-permute-start.28 = (bf16[256,2048]{1,0:T(8,128)(2,1)S(1)}, bf16[256,2048]{1,0:T(8,128)(2,1)}, u32[]{:S(2)}, u32[]{:S(2)}) collective-permute-start(bf16[256,2048]{1,0:T(8,128)(2,1)S(1)} %multiply_convert_fusion.refs_0_), channel_id=1, source_target_pairs={{0,8},{4,12},{8,0},{12,4},{1,9},{5,13},{9,1},{13,5},{2,10},{6,14},... | collective-permute-start | bytes 3145736 | tf_op jit(solution)/shard_map/ppermute | solution.py:483
  476.8 41.3 %collective-permute-start.36 = (bf16[2048,512]{1,0:T(8,128)(2,1)}, bf16[2048,512]{1,0:T(8,128)(2,1)S(1)}, u32[]{:S(2)}, u32[]{:S(2)}) collective-permute-start(bf16[2048,512]{1,0:T(8,128)(2,1)} %get-tuple-element.147.refs_0_.refs_1_), channel_id=1, source_target_pairs={{0,2},{1,3},{4,6},{5,7},{8,10},{9,11},{12,14},{13,15}} | collective-permute-start | bytes 6291464 | tf_op jit(solution)/shard_map/ppermute | solution.py:408
  518.9 57.8 %collective-permute-start.33 = (bf16[2048,512]{1,0:T(8,128)(2,1)S(1)}, bf16[2048,512]{1,0:T(8,128)(2,1)}, u32[]{:S(2)}, u32[]{:S(2)}) collective-permute-start(bf16[2048,512]{1,0:T(8,128)(2,1)S(1)} %copy-done), channel_id=1, source_target_pairs={{0,2},{1,3},{4,6},{5,7},{8,10},{9,11},{12,14},{13,15}} | collective-permute-start | bytes 6291464 | tf_op jit(solution)/shard_map/ppermute | solution.py:408
  592.9 50.4 %collective-permute-start.51 = (bf16[2048,1024]{1,0:T(8,128)(2,1)}, bf16[2048,1024]{1,0:T(8,128)(2,1)}, u32[]{:S(2)}, u32[]{:S(2)}) collective-permute-start(bf16[2048,1024]{1,0:T(8,128)(2,1)} %pad_maximum_fusion.1), channel_id=1, source_target_pairs={{0,1},{1,0},{2,3},{3,2},{4,5},{5,4},{6,7},{7,6},{8,9},{9,8},{10,11... | collective-permute-start | bytes 12582920 | tf_op jit(solution)/shard_map/ppermute | solution.py:358
  592.9 101.0 %collective-permute-start.53 = (bf16[4,688,2048]{2,1,0:T(8,128)(2,1)}, bf16[4,688,2048]{2,1,0:T(8,128)(2,1)}, u32[]{:S(2)}, u32[]{:S(2)}) collective-permute-start(bf16[4,688,2048]{2,1,0:T(8,128)(2,1)} %bitcast.46), channel_id=1, source_target_pairs={{0,1},{1,0},{2,3},{3,2},{4,5},{5,4},{6,7},{7,6},{8,9},{9,8},{10,11... | collective-permute-start | bytes 33816584 | tf_op jit(solution)/shard_map/ppermute | solution.py:358
  659.1 32.3 %collective-permute-start.54 = (bf16[4,688,1024]{2,1,0:T(8,128)(2,1)S(1)}, bf16[4,688,1024]{2,1,0:T(8,128)(2,1)S(1)}, u32[]{:S(2)}, u32[]{:S(2)}) collective-permute-start(bf16[4,688,1024]{2,1,0:T(8,128)(2,1)S(1)} %bitcast.55), channel_id=1, source_target_pairs={{0,1},{1,0},{2,3},{3,2},{4,5},{5,4},{6,7},{7,6},{8,9},{9,8},{10,11... | collective-permute-start | bytes 16908296 | tf_op jit(solution)/shard_map/ppermute | solution.py:358
  661.1 63.0 %collective-permute-start.52 = (bf16[256,2048]{1,0:T(8,128)(2,1)}, bf16[256,2048]{1,0:T(8,128)(2,1)}, u32[]{:S(2)}, u32[]{:S(2)}) collective-permute-start(bf16[256,2048]{1,0:T(8,128)(2,1)} %get-tuple-element.216), channel_id=1, source_target_pairs={{0,2},{1,3},{2,0},{3,1},{4,6},{5,7},{6,4},{7,5},{8,10},{9,11},{10,... | collective-permute-start | bytes 3145736 | tf_op jit(solution)/shard_map/ppermute | solution.py:456
  691.4 59.2 %collective-permute-start.56 = (bf16[256,2048]{1,0:T(8,128)(2,1)}, bf16[256,2048]{1,0:T(8,128)(2,1)S(1)}, u32[]{:S(2)}, u32[]{:S(2)}) collective-permute-start(bf16[256,2048]{1,0:T(8,128)(2,1)} %get-tuple-element.215), channel_id=1, source_target_pairs={{0,2},{1,3},{2,0},{3,1},{4,6},{5,7},{6,4},{7,5},{8,10},{9,11},{10,... | collective-permute-start | bytes 3145736 | tf_op jit(solution)/shard_map/ppermute | solution.py:456
  741.9 31.4 %collective-permute-start.55 = (bf16[256,2048]{1,0:T(8,128)(2,1)}, bf16[256,2048]{1,0:T(8,128)(2,1)}, u32[]{:S(2)}, u32[]{:S(2)}) collective-permute-start(bf16[256,2048]{1,0:T(8,128)(2,1)} %shard_map.194), channel_id=1, source_target_pairs={{0,2},{1,3},{2,0},{3,1},{4,6},{5,7},{6,4},{7,5},{8,10},{9,11},{10,... | collective-permute-start | bytes 3145736 | tf_op jit(solution)/shard_map/ppermute | solution.py:465
  769.8 25.6 %collective-permute-start.59 = (bf16[256,2048]{1,0:T(8,128)(2,1)}, bf16[256,2048]{1,0:T(8,128)(2,1)}, u32[]{:S(2)}, u32[]{:S(2)}) collective-permute-start(bf16[256,2048]{1,0:T(8,128)(2,1)} %shard_map.195), channel_id=1, source_target_pairs={{0,2},{1,3},{2,0},{3,1},{4,6},{5,7},{6,4},{7,5},{8,10},{9,11},{10,... | collective-permute-start | bytes 3145736 | tf_op jit(solution)/shard_map/ppermute | solution.py:468
  801.9 40.0 %collective-permute-start.60 = (bf16[256,2048]{1,0:T(8,128)(2,1)S(1)}, bf16[256,2048]{1,0:T(8,128)(2,1)S(1)}, u32[]{:S(2)}, u32[]{:S(2)}) collective-permute-start(bf16[256,2048]{1,0:T(8,128)(2,1)S(1)} %add_convert_fusion.refs_0_), channel_id=1, source_target_pairs={{0,4},{4,0},{8,12},{12,8},{1,5},{5,1},{9,13},{13,9},{2,6},{6,2},{1... | collective-permute-start | bytes 3145736 | tf_op jit(solution)/shard_map/ppermute | solution.py:482
  803.2 38.6 %collective-permute-start.61 = (bf16[256,2048]{1,0:T(8,128)(2,1)S(1)}, bf16[256,2048]{1,0:T(8,128)(2,1)S(1)}, u32[]{:S(2)}, u32[]{:S(2)}) collective-permute-start(bf16[256,2048]{1,0:T(8,128)(2,1)S(1)} %add_convert_fusion.refs_0_), channel_id=1, source_target_pairs={{0,8},{4,12},{8,0},{12,4},{1,9},{5,13},{9,1},{13,5},{2,10},{6,14},... | collective-permute-start | bytes 3145736 | tf_op jit(solution)/shard_map/ppermute | solution.py:483
  805.0 32.3 %collective-permute-start.62 = (bf16[128,2048]{1,0:T(8,128)(2,1)S(1)}, bf16[128,2048]{1,0:T(8,128)(2,1)S(1)}, u32[]{:S(2)}, u32[]{:S(2)}) collective-permute-start(bf16[128,2048]{1,0:T(8,128)(2,1)S(1)} %slice.105), channel_id=1, source_target_pairs={{0,8},{4,12},{8,0},{12,4},{1,9},{5,13},{9,1},{13,5},{2,10},{6,14},... | collective-permute-start | bytes 1572872 | tf_op jit(solution)/shard_map/ppermute | solution.py:491
  807.4 29.9 %collective-permute-start.63 = (bf16[128,2048]{1,0:T(8,128)(2,1)S(1)}, bf16[128,2048]{1,0:T(8,128)(2,1)S(1)}, u32[]{:S(2)}, u32[]{:S(2)}) collective-permute-start(bf16[128,2048]{1,0:T(8,128)(2,1)S(1)} %slice.106), channel_id=1, source_target_pairs={{0,4},{4,0},{8,12},{12,8},{1,5},{5,1},{9,13},{13,9},{2,6},{6,2},{1... | collective-permute-start | bytes 1572872 | tf_op jit(solution)/shard_map/ppermute | solution.py:491
  (106 other events, 948.7 us)
Sparse Core Ops, SparseCore 0:
  10.4 51.6 all-gather.14
  63.9 107.7 all-gather.10
  174.0 77.0 all-gather.16
  252.7 87.4 all-gather.18
  341.9 69.3 all-gather.12
  473.9 107.1 all-gather.20
